TPU v7x, 32 devices: a whole 2x2x4 slice. The times are simulated.
32 devices in a mesh: tm: 8 (over z, x), env: 4 (over y, core).
Axes of the slice: x: 2, y: 2, z: 4, core: 2. Of those that a mesh axis runs over, the one named last changes fastest.
Arguments:
- init_state: float32 [70, 1024], P(None, 'env'), may hold values from -6 to 6
- torque: float32 [32, 35, 1024], P('tm', None, 'env'), may hold values from -192 to 192
- contact: int32 [32, 1024], P('tm', 'env'), may hold values 0 or 1
- mass_inverse: float32 [16, 35, 35], P('tm'), may hold values from -0.014 to 1.5, as said below
- stiffness: float32 [35], replicated, may hold values from 10 to 100
- damping: float32 [35], replicated, may hold values from 0.5 to 5
- gravity: float32 [35], replicated, may hold values from 1 to 10
- contact_stiffness: float32 [35], replicated, may hold values from 20 to 100
- contact_damping: float32 [35], replicated, may hold values from 0.5 to 3
Outputs:
- final_states: float32 [16, 70, 1024], P('tm', None, 'env')
- corrections: float32 [3, 1024], P(None, 'env')
Inputs may be any that keep to these rules, and one draw needn't show every extreme that they name: `mass_inverse`: each matrix is symmetric, and each diagonal entry exceeds the sum of the magnitudes of the other entries of its row.
All inputs are finite; a program needn't handle non-finite values. No bound on the sum of `contact` on one device may be relied on, other than what follows from the above.
Results may differ from a plain program's by a relative error of at most 0.00025.
Values sent between devices are 32-bit elements; how exact they have to be, the bound alone decides.
A program may use at most 64 MiB of HBM per device.

v0:
```python
import functools
import math

import jax
import jax.numpy as jnp
from jax import lax
from jax.experimental import pallas as pl
from jax.experimental.pallas import tpu as pltpu
from jax.sharding import PartitionSpec as P

DOF = 35
HS = 2
SUB = 32
ITERS = 3
LANES = 128
WIDE = 256

step_length = 0.05
fine_dt = step_length / SUB
TWO_PI = 2.0 * math.pi
MESH = pl.DeviceIdType.MESH
F32 = jnp.float32
BF16 = jnp.bfloat16

SIN = (
    6.283182818551188, -41.341421398631915, 81.59618387021051,
    -76.58010048603072, 41.205394649903326, -12.271261959178284,
)


def exchange_in(tm, env, tx, m2, row, rx, mall, rows, tsend, trecv, msend, mrecv, rsend, rrecv):
    me_t = lax.axis_index("tm")
    me_e = lax.axis_index("env")
    barrier = pltpu.get_barrier_semaphore()

    def peer(k):
        return {
            "tm": lax.rem(me_t + k // env, tm),
            "env": lax.rem(me_e + lax.rem(k, env), env),
        }

    @pl.loop(1, tm * env)
    def _(k):
        pl.semaphore_signal(barrier, inc=1, device_id=peer(k), device_id_type=MESH)

    pl.semaphore_wait(barrier, tm * env - 1)

    def row_copy(k):
        return pltpu.make_async_remote_copy(
            src_ref=row,
            dst_ref=rows.at[me_t, me_e],
            send_sem=rsend.at[k],
            recv_sem=rrecv.at[k],
            device_id=peer(k),
            device_id_type=MESH,
        )

    def pair(k):
        dst = lax.rem(me_t + k, tm)
        return (
            pltpu.make_async_remote_copy(
                src_ref=m2,
                dst_ref=mall.at[me_t],
                send_sem=msend.at[k],
                recv_sem=mrecv.at[k],
                device_id={"tm": dst, "env": me_e},
                device_id_type=MESH,
            ),
            pltpu.make_async_remote_copy(
                src_ref=tx.at[dst],
                dst_ref=rx.at[me_t],
                send_sem=tsend.at[k],
                recv_sem=trecv.at[k],
                device_id={"tm": dst, "env": me_e},
                device_id_type=MESH,
            ),
        )

    @pl.loop(1, tm * env)
    def _(k):
        row_copy(k).start()

    @pl.loop(1, tm)
    def _(k):
        first, second = pair(k)
        first.start()
        second.start()

    rows[me_t, me_e] = row[...]
    mall[me_t] = m2[...]
    rx[me_t] = tx[me_t]

    @pl.loop(1, tm * env)
    def _(k):
        row_copy(k).wait()

    @pl.loop(1, tm)
    def _(k):
        first, second = pair(k)
        first.wait()
        second.wait()


def exchange_out(tm, tx, rx, send, recv):
    me_t = lax.axis_index("tm")
    me_e = lax.axis_index("env")
    barrier = pltpu.get_barrier_semaphore()

    @pl.loop(1, tm)
    def _(k):
        dst = lax.rem(me_t + k, tm)
        pl.semaphore_signal(
            barrier, inc=1, device_id={"tm": dst, "env": me_e}, device_id_type=MESH
        )

    pl.semaphore_wait(barrier, tm - 1)

    def copy(k):
        dst = lax.rem(me_t + k, tm)
        return pltpu.make_async_remote_copy(
            src_ref=tx.at[dst],
            dst_ref=rx.at[me_t],
            send_sem=send.at[k],
            recv_sem=recv.at[k],
            device_id={"tm": dst, "env": me_e},
            device_id_type=MESH,
        )

    @pl.loop(1, tm)
    def _(k):
        copy(k).start()

    rx[me_t] = tx[me_t]

    @pl.loop(1, tm)
    def _(k):
        copy(k).wait()


def split(value):
    high = value.astype(BF16)
    return high, (value - high.astype(F32)).astype(BF16)


def dot(left, right):
    return jnp.dot(left, right, preferred_element_type=F32)


class Plan:
    def __init__(self, slices):
        per = LANES // DOF
        self.groups = []
        self.where = []
        base = 0
        for first in range(0, slices, per):
            count = min(per, slices - first)
            width = -(-count * DOF // LANES) * LANES
            self.groups.append((base, width, first, count))
            for pos in range(count):
                self.where.append(base + pos * DOF)
            base += width
        self.lanes = base


def compute(
    slices, local, total_env,
    rx, mall, rows, stiff, damp, gravity, cstiff, cdamp,
    out,
    tq, spring, fric, grav, cspring, cfric, wgt, wtmp, ybuf, ubuf, by, bu, ly, lu, cmap, pmap, ctmp, xs,
):
    plan = Plan(slices)
    epd = rx.shape[1]
    ratio = float(SUB)
    block = 4 if slices % 4 == 0 else 1
    unroll = max(1, min(SUB, 96 // len(plan.groups)))
    stiff, damp, gravity, cstiff, cdamp = (r[...] for r in (stiff, damp, gravity, cstiff, cdamp))
    to_u = TWO_PI / fine_dt

    for ref in (tq, spring, fric, grav, cspring, cfric, ybuf, ubuf, ly, lu):
        ref[...] = jnp.zeros(ref.shape, ref.dtype)
    ctmp[...] = jnp.zeros(ctmp.shape, F32)
    xs[...] = jnp.zeros(xs.shape, F32)

    sums = jnp.sum(rows[...], axis=1)[:, 0, :] * (1.0 / total_env)
    for n in range(slices):
        src, pos = divmod(n, local)
        at = plan.where[n]
        cut = pl.ds(at, DOF)
        grav[:, cut] = jnp.broadcast_to(gravity, (1, DOF))
        for j in range(HS):
            step = pos * HS + j
            lane = local * HS * DOF + step
            hit = rx[src, :, lane : lane + 1]
            mean = sums[src : src + 1, step : step + 1]
            tq[j, :, cut] = rx[src, :, step * DOF : (step + 1) * DOF]
            spring[j, :, cut] = TWO_PI * (stiff + hit * cstiff)
            fric[j, :, cut] = to_u * (damp + hit * cdamp)
            cspring[j, :, cut] = TWO_PI * (stiff + gravity + mean * cstiff)
            cfric[j, :, cut] = to_u * (damp + mean * cdamp)

    for g, (base, width, first, count) in enumerate(plan.groups):
        wtmp[...] = jnp.zeros(wtmp.shape, F32)
        for pos in range(count):
            src, here = divmod(first + pos, local)
            wtmp[pl.ds(pos * DOF, DOF), pl.ds(pos * DOF, DOF)] = (
                fine_dt * fine_dt / TWO_PI
            ) * mall[src, :, here * DOF : (here + 1) * DOF]
        high, low = split(wtmp[...])
        wgt[g, 0:LANES, 0:LANES] = high
        wgt[g, LANES:, 0:LANES] = high
        wgt[g, 0:LANES, LANES:] = low
        wgt[g, LANES:, LANES:] = jnp.zeros_like(low)

    def product(force, g, width):
        high, low = split(force)
        both = dot(jnp.concatenate([high, low], axis=1), wgt[g])
        return both[:, :LANES] + both[:, LANES:]

    rank = lax.broadcasted_iota(jnp.int32, (ly.shape[0], DOF), 0)
    col = lax.broadcasted_iota(jnp.int32, (ly.shape[0], DOF), 1)
    for n in range(slices):
        cut = pl.ds(plan.where[n], DOF)
        ly[:, cut] = jnp.where(rank == col, 1.0, 0.0)
        lu[:, cut] = jnp.where(rank == col + DOF, 1.0, 0.0)
    for g, (base, width, first, count) in enumerate(plan.groups):
        cut = pl.ds(base, width)
        y, u = ly[:, cut], lu[:, cut]
        for j in range(HS):
            force = -cspring[j, :, cut] * y - cfric[j, :, cut] * u
            u = u + ratio * product(force, g, width)
            y = y + ratio * u
        ly[:, cut] = y
        lu[:, cut] = u
        u = ratio * product(tq[0, :, cut], g, width)
        y = ratio * u
        for j in range(1, HS):
            force = tq[j, :, cut] - cspring[j, :, cut] * y - cfric[j, :, cut] * u
            u = u + ratio * product(force, g, width)
            y = y + ratio * u
        by[:, cut] = y
        bu[:, cut] = u
    cmap[...] = jnp.zeros(cmap.shape, BF16)
    depth = ly.shape[0]
    for n in range(slices):
        cut = pl.ds(plan.where[n], DOF)
        ctmp[0:depth, 0:DOF] = ly[:, cut]
        ctmp[0:depth, DOF : 2 * DOF] = lu[:, cut]
        high, low = split(ctmp[...])
        cmap[n, 0:LANES, 0:LANES] = high
        cmap[n, LANES:, 0:LANES] = high
        cmap[n, 0:LANES, LANES:] = low

    def through(state, weight):
        high, low = split(state)
        both = dot(jnp.concatenate([high, low], axis=1), weight)
        return both[:, :LANES] + both[:, LANES:]

    firsts = range(0, slices, block)
    running = {m: jnp.concatenate(
        [ly[:, pl.ds(plan.where[m], DOF)], lu[:, pl.ds(plan.where[m], DOF)],
         jnp.zeros((depth, LANES - 2 * DOF), F32)], axis=1) for m in firsts}
    for i in range(1, block):
        for m in firsts:
            running[m] = through(running[m], cmap[m + i])
            ctmp[0:depth, :] = running[m]
            high, low = split(ctmp[...])
            pmap[m + i, 0:LANES, 0:LANES] = high
            pmap[m + i, LANES:, 0:LANES] = high
            pmap[m + i, 0:LANES, LANES:] = low
            pmap[m + i, LANES:, LANES:] = jnp.zeros_like(low)

    def sweep(offsets, entry):
        ends = list(offsets)
        for i in range(1, block):
            for m in firsts:
                ends[m + i] = through(ends[m + i - 1], cmap[m + i]) + ends[m + i]
        enter = {}
        for m in firsts:
            enter[m] = entry
            last = m + block - 1
            whole = pmap if block > 1 else cmap
            if entry is not None:
                ends[last] = ends[last] + through(entry, whole[last])
            entry = ends[last]
        for i in range(block - 1):
            for m in firsts:
                if enter[m] is not None:
                    part = cmap if i == 0 else pmap
                    ends[m + i] = ends[m + i] + through(enter[m], part[m + i])
        return ends

    def packed(yref, uref, n):
        cut = pl.ds(plan.where[n], DOF)
        zero = jnp.zeros((epd, LANES - 2 * DOF), F32)
        return jnp.concatenate([yref[:, cut], uref[:, cut], zero], axis=1)

    lane_of = lax.broadcasted_iota(jnp.int32, (1, LANES), 1)
    scale = jnp.where(lane_of < DOF, TWO_PI, to_u)
    shrink = jnp.where(lane_of < DOF, 1.0 / TWO_PI, 1.0 / to_u)
    first_lane = local * HS * (DOF + 1)
    own = rx[lax.axis_index("tm")][:, first_lane : first_lane + 2 * DOF]
    state = jnp.concatenate([own, jnp.zeros((epd, LANES - 2 * DOF), F32)], axis=1) * shrink
    xs[0] = state
    ends = sweep([packed(by, bu, n) for n in range(slices)], state)
    for n in range(slices):
        xs[n + 1] = ends[n]

    def iteration(k, corrections):
        for n in range(slices):
            cut = pl.ds(plan.where[n], DOF)
            ybuf[:, cut] = xs[n, :, 0:DOF]
            ubuf[:, cut] = xs[n, :, DOF : 2 * DOF]
        for j in range(HS):

            def substep(counter, carry):
                result = []
                for g, (base, width, first, count) in enumerate(plan.groups):
                    y, u = carry[g]
                    cut = pl.ds(base, width)
                    t = y - jnp.round(y)
                    s = t * t
                    poly = jnp.full_like(s, SIN[-1])
                    for c in SIN[-2::-1]:
                        poly = poly * s + c
                    force = (
                        tq[j, :, cut]
                        - spring[j, :, cut] * y
                        - fric[j, :, cut] * u
                        - (grav[:, cut] * t) * poly
                    )
                    u = u + product(force, g, width)
                    y = y + u
                    result.append((y, u))
                return tuple(result)

            first_state = tuple(
                (ybuf[:, pl.ds(base, width)], ubuf[:, pl.ds(base, width)])
                for base, width, first, count in plan.groups
            )
            last = lax.fori_loop(0, SUB, substep, first_state, unroll=unroll)
            for g, (base, width, first, count) in enumerate(plan.groups):
                ybuf[:, pl.ds(base, width)] = last[g][0]
                ubuf[:, pl.ds(base, width)] = last[g][1]
        worst = jnp.zeros((epd, 1), F32)
        changes = sweep([packed(ybuf, ubuf, n) - xs[n + 1] for n in range(slices)], None)
        for n in range(slices):
            real = changes[n] * scale
            worst = jnp.maximum(worst, jnp.sum(real * real, axis=1, keepdims=True))
            xs[n + 1] = xs[n + 1] + changes[n]
        return jnp.where(lane_of == k, jnp.sqrt(worst), corrections)

    corrections = lax.fori_loop(0, ITERS, iteration, jnp.zeros((epd, LANES), F32))
    rows_of = 2 * DOF
    for n in range(slices):
        dst, pos = divmod(n, local)
        out[dst, :, pos * rows_of : (pos + 1) * rows_of] = (xs[n + 1] * scale)[:, :rows_of]
    for dst in range(slices // local):
        out[dst, :, local * rows_of : local * rows_of + ITERS] = corrections[:, :ITERS]


def body(tm, env, init_state, torque, contact, mass_inverse, stiffness, damping, gravity,
         contact_stiffness, contact_damping):
    local = mass_inverse.shape[0]
    steps = torque.shape[0]
    env_local = init_state.shape[1]
    epd = env_local // tm
    slices = local * tm
    plan = Plan(slices)
    vmem = pl.BlockSpec(memory_space=pltpu.VMEM)
    dma = pltpu.SemaphoreType.DMA

    flat = jnp.concatenate(
        [torque.reshape(steps * DOF, env_local), contact.astype(F32), init_state], axis=0
    ).T
    wide = flat.shape[1]
    tx = flat.reshape(tm, epd, wide)
    m2 = mass_inverse.transpose(1, 0, 2).reshape(DOF, local * DOF)
    row = jnp.pad(jnp.sum(contact.astype(F32), axis=1)[None], ((0, 0), (0, LANES - steps)))
    rx, mall, rows = pl.pallas_call(
        functools.partial(exchange_in, tm, env),
        out_shape=(
            jax.ShapeDtypeStruct(tx.shape, F32),
            jax.ShapeDtypeStruct((tm,) + m2.shape, F32),
            jax.ShapeDtypeStruct((tm, env, 1, LANES), F32),
        ),
        in_specs=[vmem] * 3,
        out_specs=(vmem,) * 3,
        scratch_shapes=[dma((tm,))] * 4 + [dma((tm * env,))] * 2,
        compiler_params=pltpu.CompilerParams(collective_id=0, has_side_effects=True),
        name="exchange_in",
    )(tx, m2, row)

    prm = [p.reshape(1, DOF) for p in (stiffness, damping, gravity, contact_stiffness, contact_damping)]
    depth = -(-2 * DOF // 8) * 8
    lanes = plan.lanes
    groups = len(plan.groups)
    width_out = local * 2 * DOF + ITERS
    big = pltpu.VMEM((epd, lanes), F32)
    both = pltpu.VMEM((HS, epd, lanes), F32)
    thin = pltpu.VMEM((HS, 1, lanes), F32)
    out = pl.pallas_call(
        functools.partial(compute, slices, local, env_local * env),
        out_shape=jax.ShapeDtypeStruct((tm, epd, width_out), F32),
        in_specs=[vmem] * 8,
        out_specs=vmem,
        scratch_shapes=[
            both, both, both, pltpu.VMEM((1, lanes), F32), thin, thin,
            pltpu.VMEM((groups, WIDE, WIDE), BF16),
            pltpu.VMEM((LANES, LANES), F32),
            big, big, big, big,
            pltpu.VMEM((depth, lanes), F32), pltpu.VMEM((depth, lanes), F32),
            pltpu.VMEM((slices, 2 * LANES, 2 * LANES), BF16),
            pltpu.VMEM((slices, 2 * LANES, 2 * LANES), BF16),
            pltpu.VMEM((LANES, LANES), F32),
            pltpu.VMEM((slices + 1, epd, LANES), F32),
        ],
        name="parareal",
    )(rx, mall, rows, *prm)

    back = pl.pallas_call(
        functools.partial(exchange_out, tm),
        out_shape=jax.ShapeDtypeStruct(out.shape, F32),
        in_specs=[vmem],
        out_specs=vmem,
        scratch_shapes=[dma((tm,))] * 2,
        compiler_params=pltpu.CompilerParams(collective_id=1, has_side_effects=True),
        name="exchange_out",
    )(out)
    turned = back.reshape(env_local, width_out).T
    states = turned[: local * 2 * DOF].reshape(local, 2 * DOF, env_local)
    return states, turned[local * 2 * DOF :]


def solution(mesh):
    placed = (
        P(None, "env"),
        P("tm", None, "env"),
        P("tm", "env"),
        P("tm", None, None),
        P(),
        P(),
        P(),
        P(),
        P(),
    )
    return jax.shard_map(
        functools.partial(body, mesh.shape["tm"], mesh.shape["env"]),
        mesh=mesh,
        in_specs=placed,
        out_specs=(P("tm", None, "env"), P(None, "env")),
        check_vma=False,
    )
```

profile of v0, /device:TPU:0, one launch (start us, length us, event | category | flops | bytes accessed | tf_op | source)
XLA Modules:
  0.0 75.9 jit_solution(16470762958396341117)
XLA Ops:
  0.6 0.0 copy-start.1
  0.6 0.7 copy-done.1
  1.3 0.1 convert_reduce_fusion
  1.4 0.5 pad.4.row
  2.0 1.5 %reshape.36.m2 = f32[35,70]{1,0:T(8,128)} reshape(f32[35,2,35]{2,1,0:T(2,128)} %bitcast.17) | data formatting | bytes 19600 | tf_op jit(solution)/shard_map/reshape | solution.py:377
  3.4 0.9 %copy.14 = f32[4,35,256]{2,1,0:T(8,128)S(1)} copy(f32[4,35,256]{2,0,1:T(4,128)} %param.10) | data formatting | bytes 286720 | tf_op args[1]
  4.4 0.0 copy-start
  4.4 0.8 %copy-done = f32[70,256]{1,0:T(8,128)S(1)} copy-done((f32[70,256]{1,0:T(8,128)S(1)}, f32[70,256]{1,0:T(8,128)}, u32[]{:S(2)}) %copy-start) | copy-done | bytes 71704
  5.3 0.8 %copy.15 = f32[256,214]{1,0:T(8,128)} copy(f32[256,214]{0,1:T(8,128)S(1)} %maximum_bitcast_fusion) | data formatting | bytes 438272 | tf_op jit(solution)/shard_map/transpose | solution.py:374
  6.1 17.4 %exchange_in.1 = (f32[8,32,214]{2,1,0:T(8,128)}, f32[8,35,70]{2,1,0:T(8,128)}, f32[8,4,1,128]{3,2,1,0:T(1,128)}) custom-call(f32[8,32,214]{2,1,0:T(8,128)} %bitcast.14, f32[35,70]{1,0:T(8,128)} %reshape.36.m2, f32[1,128]{1,0:T(1,128)} %pad.4.row), custom_call_target="tpu_custom_call" | custom-call | tf_op jit(solution)/shard_map/exchange_in/pallas_call | solution.py:379
  23.5 37.2 %parareal.1.tx = f32[8,32,143]{2,1,0:T(8,128)} custom-call(f32[8,32,214]{2,1,0:T(8,128)} %get-tuple-element.5.rx, f32[8,35,70]{2,1,0:T(8,128)} %get-tuple-element.6.mall, f32[8,4,1,128]{3,2,1,0:T(1,128)} %get-tuple-element.7.rows, f32[1,35]{1,0:T(1,128)} %bitcast.18, f32[1,35]{1,0:T(1,128)} %bitcast.19, f32[1,35]{1,0:T(1,128)} %bitcast.20, ...), custom_call_target="tpu_custom_call" | custom-call | tf_op jit(solution)/shard_map/parareal/pallas_call | solution.py:401
  60.7 12.7 %exchange_out.1 = f32[8,32,143]{2,1,0:T(8,128)} custom-call(f32[8,32,143]{2,1,0:T(8,128)} %parareal.1.tx), custom_call_target="tpu_custom_call" | custom-call | tf_op jit(solution)/shard_map/exchange_out/pallas_call | solution.py:420
  73.5 1.0 %copy.16 = f32[256,143]{0,1:T(8,128)S(1)} copy(f32[256,143]{1,0:T(8,128)} %bitcast.13) | data formatting | bytes 292864 | tf_op jit(solution)/shard_map/reshape | solution.py:429
  74.5 0.6 slice.9
  75.1 0.7 copy.17
  (4 shorter events, 0.1 us)
Async XLA Ops:
  0.6 0.7 copy-start.1
  4.4 0.9 %copy-start = (f32[70,256]{1,0:T(8,128)S(1)}, f32[70,256]{1,0:T(8,128)}, u32[]{:S(2)}) copy-start(f32[70,256]{1,0:T(8,128)} %param.9) | copy-start | bytes 215044
where the time goes:
time: 76.2 us; the launch traced here: 75.9 us
  Pallas kernels  67.3 us (88%)
  local copies, waits for them, and re-layouts  7.69 us (10%)
    pallas_call x1, Pallas kernels, body(): pl.pallas_call(functools.partial(compute, slices, local, env_local * env)...  37.2 us
    pallas_call x1, Pallas kernels, body(): pl.pallas_call(functools.partial(exchange_in, tm, env), out_shape=(jax.Sh...  17.4 us
    pallas_call x1, Pallas kernels, body(): pl.pallas_call(functools.partial(exchange_out, tm), out_shape=jax.ShapeDt...  12.7 us
    unnamed x6, local copies, waits for them, and re-layouts  3.2 us

commit v1 on v0

v1 whole, which is shorter than its diff:
```python
import functools
import math

import jax
import jax.numpy as jnp
from jax import lax
from jax.experimental import pallas as pl
from jax.experimental.pallas import tpu as pltpu
from jax.sharding import PartitionSpec as P

DOF = 35
HS = 2
SUB = 32
ITERS = 3
LANES = 128
WIDE = 256
VOFF = -(-DOF // 8) * 8
DEPTH = 2 * VOFF
PER = LANES // DOF
SPARE = PER * DOF

step_length = 0.05
fine_dt = step_length / SUB
TWO_PI = 2.0 * math.pi
MESH = pl.DeviceIdType.MESH
F32 = jnp.float32
BF16 = jnp.bfloat16

SIN = (
    6.283182818551188, -41.341421398631915, 81.59618387021051,
    -76.58010048603072, 41.205394649903326, -12.271261959178284,
)


def up8(n):
    return -(-n // 8) * 8


def split(value):
    high = value.astype(BF16)
    return high, (value - high.astype(F32)).astype(BF16)


def dot(left, right):
    return jnp.dot(left, right, preferred_element_type=F32)


class Plan:
    def __init__(self, slices):
        per = PER
        self.groups = []
        self.where = []
        base = 0
        for first in range(0, slices, per):
            count = min(per, slices - first)
            width = -(-count * DOF // LANES) * LANES
            self.groups.append((base, width, first, count))
            for pos in range(count):
                self.where.append(base + pos * DOF)
            base += width
        self.lanes = base


class Message:
    def __init__(self, steps, local, epd):
        self.steps, self.local, self.epd = steps, local, epd
        count = steps + local
        self.tiles = -(-count // PER)
        self.rows = []
        self.start = []
        base = 0
        for tile in range(self.tiles):
            pieces = range(tile * PER, min(count, (tile + 1) * PER))
            tall = any(i >= steps for i in pieces)
            rows = max(up8(epd), up8(DOF)) if tall else up8(epd)
            self.start.append(base)
            self.rows.append(rows)
            base += rows
        self.total = base

    def place(self, piece):
        tile, pos = divmod(piece, PER)
        return self.start[tile], pos * DOF


def kernel(
    tm, env, local, total_env,
    init, torque, contact, minv, stiff_r, damp_r, gravity_r, cstiff_r, cdamp_r,
    states_out, corr_out,
    tx, rx, row, rows, srow, sums, otx, orx, turn, mtile, own,
    tq, spring, fric, grav, cspring, cfric, wgt, wtmp, ybuf, ubuf, by, bu, ly, lu, cmap, pmap, ctmp, xs,
    tsend, trecv, esend, erecv, ssend, srecv, osend, orecv,
):
    slices = local * tm
    steps = local * HS
    env_local = contact.shape[1]
    epd = env_local // tm
    plan = Plan(slices)
    msg = Message(steps, local, epd)
    me_t = lax.axis_index("tm")
    me_e = lax.axis_index("env")
    barrier = pltpu.get_barrier_semaphore()

    def tm_peer(k):
        return {"tm": lax.rem(me_t + k, tm), "env": me_e}

    def env_peer(k):
        return {"tm": me_t, "env": lax.rem(me_e + k, env)}

    for k in range(1, env):
        pl.semaphore_signal(barrier, inc=1, device_id=env_peer(k), device_id_type=MESH)
    for k in range(1, tm):
        pl.semaphore_signal(barrier, inc=1, device_id=tm_peer(k), device_id_type=MESH)

    hits = contact[...].astype(F32)
    row[...] = jnp.zeros(row.shape, F32)
    row[0:steps, :] = jnp.broadcast_to(jnp.sum(hits, axis=1, keepdims=True), (steps, LANES))
    for tile in range(msg.tiles):
        turn[...] = jnp.zeros(turn.shape, F32)
        mtile[...] = jnp.zeros(mtile.shape, F32)
        for pos in range(PER):
            piece = tile * PER + pos
            if piece < steps:
                turn[pos * DOF : (pos + 1) * DOF, :] = torque[:, piece, :]
            elif piece < steps + local:
                mtile[0:DOF, pos * DOF : (pos + 1) * DOF] = minv[:, piece - steps, :]
        if tile == 0:
            turn[SPARE : SPARE + steps, :] = hits
        turned = turn[...].T
        first, count = msg.start[tile], msg.rows[tile]
        tall = count > up8(epd) or any(
            steps <= i < steps + local for i in range(tile * PER, (tile + 1) * PER))
        for p in range(tm):
            chunk = turned[p * epd : (p + 1) * epd]
            if tall:
                tx[p, first : first + count, :] = mtile[0:count, :]
                tx[p, first : first + epd, :] = tx[p, first : first + epd, :] + chunk
            else:
                tx[p, first : first + epd, :] = chunk
    turn[...] = jnp.zeros(turn.shape, F32)
    turn[0:DOF, :] = init[0:DOF, :]
    turn[VOFF : VOFF + DOF, :] = init[DOF : 2 * DOF, :]
    turned = turn[...].T
    for p in range(tm):
        own[p] = turned[p * epd : (p + 1) * epd]

    pl.semaphore_wait(barrier, tm + env - 2)

    def row_copy(k):
        return pltpu.make_async_remote_copy(
            src_ref=row, dst_ref=rows.at[me_e], send_sem=esend.at[k], recv_sem=erecv.at[k],
            device_id=env_peer(k), device_id_type=MESH)

    def block_copy(k):
        return pltpu.make_async_remote_copy(
            src_ref=tx.at[lax.rem(me_t + k, tm)], dst_ref=rx.at[me_t],
            send_sem=tsend.at[k], recv_sem=trecv.at[k],
            device_id=tm_peer(k), device_id_type=MESH)

    def sum_copy(k):
        return pltpu.make_async_remote_copy(
            src_ref=srow, dst_ref=sums.at[me_t], send_sem=ssend.at[k], recv_sem=srecv.at[k],
            device_id=tm_peer(k), device_id_type=MESH)

    def out_copy(k):
        return pltpu.make_async_remote_copy(
            src_ref=otx.at[lax.rem(me_t + k, tm)], dst_ref=orx.at[me_t],
            send_sem=osend.at[k], recv_sem=orecv.at[k],
            device_id=tm_peer(k), device_id_type=MESH)

    row_copies = [row_copy(k) for k in range(1, env)]
    block_copies = [block_copy(k) for k in range(1, tm)]
    sum_copies = [sum_copy(k) for k in range(1, tm)]
    for c in row_copies + block_copies:
        c.start()
    rows[me_e] = row[...]
    rx[me_t] = tx[me_t]

    stiff, damp, gravity, cstiff, cdamp = (
        r[...] for r in (stiff_r, damp_r, gravity_r, cstiff_r, cdamp_r))
    ratio = float(SUB)
    block = 4 if slices % 4 == 0 else 1
    unroll = max(1, min(SUB, 96 // len(plan.groups)))
    to_u = TWO_PI / fine_dt
    for ref in (tq, spring, fric, grav, cspring, cfric, ybuf, ubuf, ly, lu):
        ref[...] = jnp.zeros(ref.shape, ref.dtype)
    ctmp[...] = jnp.zeros(ctmp.shape, F32)
    xs[...] = jnp.zeros(xs.shape, F32)
    cmap[...] = jnp.zeros(cmap.shape, BF16)
    rank = lax.broadcasted_iota(jnp.int32, (DEPTH, DOF), 0)
    col = lax.broadcasted_iota(jnp.int32, (DEPTH, DOF), 1)
    for n in range(slices):
        cut = pl.ds(plan.where[n], DOF)
        grav[:, cut] = gravity
        ly[:, cut] = jnp.where(rank == col, 1.0, 0.0)
        lu[:, cut] = jnp.where(rank == col + VOFF, 1.0, 0.0)

    for c in row_copies:
        c.wait()
    srow[...] = jnp.sum(rows[...], axis=0) * (1.0 / total_env)
    for c in sum_copies:
        c.start()
    sums[me_t] = srow[...]
    for c in block_copies:
        c.wait()

    for n in range(slices):
        src, pos = divmod(n, local)
        cut = pl.ds(plan.where[n], DOF)
        for j in range(HS):
            step = pos * HS + j
            first, lane = msg.place(step)
            hit = rx[src, 0:epd, SPARE + step : SPARE + step + 1]
            tq[j, :, cut] = rx[src, first : first + epd, lane : lane + DOF]
            spring[j, :, cut] = TWO_PI * (stiff + hit * cstiff)
            fric[j, :, cut] = to_u * (damp + hit * cdamp)

    for g, (base, width, first, count) in enumerate(plan.groups):
        wtmp[...] = jnp.zeros(wtmp.shape, F32)
        for pos in range(count):
            src, here = divmod(first + pos, local)
            start, lane = msg.place(steps + here)
            wtmp[pl.ds(pos * DOF, DOF), pl.ds(pos * DOF, DOF)] = (
                fine_dt * fine_dt / TWO_PI
            ) * rx[src, start : start + DOF, lane : lane + DOF]
        high, low = split(wtmp[...])
        wgt[g, 0:LANES, 0:LANES] = high
        wgt[g, LANES:, 0:LANES] = high
        wgt[g, 0:LANES, LANES:] = low
        wgt[g, LANES:, LANES:] = jnp.zeros_like(low)

    for c in sum_copies:
        c.wait()
    for n in range(slices):
        src, pos = divmod(n, local)
        cut = pl.ds(plan.where[n], DOF)
        for j in range(HS):
            step = pos * HS + j
            mean = sums[src, step : step + 1, 0:DOF]
            cspring[j, :, cut] = TWO_PI * (stiff + gravity + mean * cstiff)
            cfric[j, :, cut] = to_u * (damp + mean * cdamp)

    def product(force, g):
        high, low = split(force)
        both = dot(jnp.concatenate([high, low], axis=1), wgt[g])
        return both[:, :LANES] + both[:, LANES:]

    for g, (base, width, first, count) in enumerate(plan.groups):
        cut = pl.ds(base, width)
        y, u = ly[:, cut], lu[:, cut]
        for j in range(HS):
            force = -cspring[j, :, cut] * y - cfric[j, :, cut] * u
            u = u + ratio * product(force, g)
            y = y + ratio * u
        ly[:, cut] = y
        lu[:, cut] = u
        u = ratio * product(tq[0, :, cut], g)
        y = ratio * u
        for j in range(1, HS):
            force = tq[j, :, cut] - cspring[j, :, cut] * y - cfric[j, :, cut] * u
            u = u + ratio * product(force, g)
            y = y + ratio * u
        by[:, cut] = y
        bu[:, cut] = u
    for n in range(slices):
        cut = pl.ds(plan.where[n], DOF)
        ctmp[0:DEPTH, 0:DOF] = ly[:, cut]
        ctmp[0:DEPTH, VOFF : VOFF + DOF] = lu[:, cut]
        high, low = split(ctmp[...])
        cmap[n, 0:LANES, 0:LANES] = high
        cmap[n, LANES:, 0:LANES] = high
        cmap[n, 0:LANES, LANES:] = low

    def through(state, weight):
        high, low = split(state)
        both = dot(jnp.concatenate([high, low], axis=1), weight)
        return both[:, :LANES] + both[:, LANES:]

    def joined(y, u, depth):
        gap = jnp.zeros((depth, VOFF - DOF), F32)
        return jnp.concatenate(
            [y, gap, u, jnp.zeros((depth, LANES - VOFF - DOF), F32)], axis=1)

    firsts = range(0, slices, block)
    running = {m: joined(ly[:, pl.ds(plan.where[m], DOF)], lu[:, pl.ds(plan.where[m], DOF)], DEPTH)
               for m in firsts}
    for i in range(1, block):
        for m in firsts:
            running[m] = through(running[m], cmap[m + i])
            ctmp[0:DEPTH, :] = running[m]
            high, low = split(ctmp[...])
            pmap[m + i, 0:LANES, 0:LANES] = high
            pmap[m + i, LANES:, 0:LANES] = high
            pmap[m + i, 0:LANES, LANES:] = low
            pmap[m + i, LANES:, LANES:] = jnp.zeros_like(low)

    def sweep(offsets, entry):
        ends = list(offsets)
        for i in range(1, block):
            for m in firsts:
                ends[m + i] = through(ends[m + i - 1], cmap[m + i]) + ends[m + i]
        enter = {}
        for m in firsts:
            enter[m] = entry
            last = m + block - 1
            whole = pmap if block > 1 else cmap
            if entry is not None:
                ends[last] = ends[last] + through(entry, whole[last])
            entry = ends[last]
        for i in range(block - 1):
            for m in firsts:
                if enter[m] is not None:
                    part = cmap if i == 0 else pmap
                    ends[m + i] = ends[m + i] + through(enter[m], part[m + i])
        return ends

    def packed(yref, uref, n):
        cut = pl.ds(plan.where[n], DOF)
        return joined(yref[:, cut], uref[:, cut], epd)

    lane_of = lax.broadcasted_iota(jnp.int32, (1, LANES), 1)
    scale = jnp.where(lane_of < VOFF, TWO_PI, to_u)
    shrink = jnp.where(lane_of < VOFF, 1.0 / TWO_PI, 1.0 / to_u)
    state = own[me_t] * shrink
    xs[0] = state
    ends = sweep([packed(by, bu, n) for n in range(slices)], state)
    for n in range(slices):
        xs[n + 1] = ends[n]

    def iteration(k, corrections):
        for n in range(slices):
            cut = pl.ds(plan.where[n], DOF)
            ybuf[:, cut] = xs[n, :, 0:DOF]
            ubuf[:, cut] = xs[n, :, VOFF : VOFF + DOF]
        for j in range(HS):

            def substep(counter, carry):
                result = []
                for g, (base, width, first, count) in enumerate(plan.groups):
                    y, u = carry[g]
                    cut = pl.ds(base, width)
                    t = y - jnp.round(y)
                    s = t * t
                    poly = jnp.full_like(s, SIN[-1])
                    for c in SIN[-2::-1]:
                        poly = poly * s + c
                    force = (
                        tq[j, :, cut]
                        - spring[j, :, cut] * y
                        - fric[j, :, cut] * u
                        - (grav[:, cut] * t) * poly
                    )
                    u = u + product(force, g)
                    y = y + u
                    result.append((y, u))
                return tuple(result)

            first_state = tuple(
                (ybuf[:, pl.ds(base, width)], ubuf[:, pl.ds(base, width)])
                for base, width, first, count in plan.groups
            )
            last = lax.fori_loop(0, SUB, substep, first_state, unroll=unroll)
            for g, (base, width, first, count) in enumerate(plan.groups):
                ybuf[:, pl.ds(base, width)] = last[g][0]
                ubuf[:, pl.ds(base, width)] = last[g][1]
        worst = jnp.zeros((epd, 1), F32)
        changes = sweep([packed(ybuf, ubuf, n) - xs[n + 1] for n in range(slices)], None)
        for n in range(slices):
            real = changes[n] * scale
            worst = jnp.maximum(worst, jnp.sum(real * real, axis=1, keepdims=True))
            xs[n + 1] = xs[n + 1] + changes[n]
        return jnp.where(lane_of == DOF + k, jnp.sqrt(worst), corrections)

    corrections = lax.fori_loop(0, ITERS, iteration, jnp.zeros((epd, LANES), F32))

    span = local * epd
    for t in range(tm):
        parts = [xs[t * local + pos + 1] * scale for pos in range(local)]
        parts[0] = parts[0] + corrections
        turned = jnp.concatenate(parts, axis=0).T
        otx[t, :, 0:span] = turned[0:VOFF]
        otx[t, :, span : 2 * span] = turned[VOFF:DEPTH]
    out_copies = [out_copy(k) for k in range(1, tm)]
    for c in out_copies:
        c.start()
    orx[me_t] = otx[me_t]
    for c in out_copies:
        c.wait()

    across = LANES // epd
    lanes = lax.broadcasted_iota(jnp.int32, (VOFF, LANES), 1)
    for part in range(2):
        for pos in range(local):
            off = part * span + pos * epd
            for tile in range(env_local // LANES):
                acc = None
                for q in range(across):
                    block_in = orx[tile * across + q]
                    shift = (q * epd - off) % LANES
                    moved = pltpu.roll(block_in, shift, 1) if shift else block_in
                    acc = moved if acc is None else jnp.where(lanes >= q * epd, moved, acc)
                cut = pl.ds(tile * LANES, LANES)
                states_out[part * DOF : (part + 1) * DOF, pos, cut] = acc[0:DOF]
                if part == 0 and pos == 0:
                    corr_out[:, cut] = acc[DOF : DOF + ITERS]


def body(tm, env, init_state, torque, contact, mass_inverse, stiffness, damping, gravity,
         contact_stiffness, contact_damping):
    local = mass_inverse.shape[0]
    env_local = init_state.shape[1]
    epd = env_local // tm
    steps = local * HS
    slices = local * tm
    plan = Plan(slices)
    msg = Message(steps, local, epd)
    vmem = pl.BlockSpec(memory_space=pltpu.VMEM)
    dma = pltpu.SemaphoreType.DMA
    prm = [p.reshape(1, DOF) for p in (stiffness, damping, gravity, contact_stiffness, contact_damping)]
    lanes = plan.lanes
    groups = len(plan.groups)
    big = pltpu.VMEM((epd, lanes), F32)
    both = pltpu.VMEM((HS, epd, lanes), F32)
    thin = pltpu.VMEM((HS, 1, lanes), F32)
    row = (up8(steps), LANES)
    states, corrections = pl.pallas_call(
        functools.partial(kernel, tm, env, local, env_local * env),
        out_shape=(
            jax.ShapeDtypeStruct((2 * DOF, local, env_local), F32),
            jax.ShapeDtypeStruct((ITERS, env_local), F32),
        ),
        in_specs=[vmem] * 9,
        out_specs=(vmem, vmem),
        scratch_shapes=[
            pltpu.VMEM((tm, msg.total, LANES), F32), pltpu.VMEM((tm, msg.total, LANES), F32),
            pltpu.VMEM(row, F32), pltpu.VMEM((env,) + row, F32),
            pltpu.VMEM(row, F32), pltpu.VMEM((tm,) + row, F32),
            pltpu.VMEM((tm, VOFF, LANES), F32), pltpu.VMEM((tm, VOFF, LANES), F32),
            pltpu.VMEM((LANES, env_local), F32),
            pltpu.VMEM((max(msg.rows), LANES), F32),
            pltpu.VMEM((tm, epd, LANES), F32),
            both, both, both, pltpu.VMEM((1, lanes), F32), thin, thin,
            pltpu.VMEM((groups, WIDE, WIDE), BF16),
            pltpu.VMEM((LANES, LANES), F32),
            big, big, big, big,
            pltpu.VMEM((DEPTH, lanes), F32), pltpu.VMEM((DEPTH, lanes), F32),
            pltpu.VMEM((slices, 2 * LANES, 2 * LANES), BF16),
            pltpu.VMEM((slices, 2 * LANES, 2 * LANES), BF16),
            pltpu.VMEM((LANES, LANES), F32),
            pltpu.VMEM((slices + 1, epd, LANES), F32),
            dma((tm,)), dma((tm,)), dma((env,)), dma((env,)),
            dma((tm,)), dma((tm,)), dma((tm,)), dma((tm,)),
        ],
        compiler_params=pltpu.CompilerParams(collective_id=0, has_side_effects=True),
        name="parareal",
    )(init_state, jnp.transpose(torque, (1, 0, 2)), contact,
      jnp.transpose(mass_inverse, (1, 0, 2)), *prm)
    return jnp.transpose(states, (1, 0, 2)), corrections


def solution(mesh):
    placed = (
        P(None, "env"),
        P("tm", None, "env"),
        P("tm", "env"),
        P("tm", None, None),
        P(),
        P(),
        P(),
        P(),
        P(),
    )
    return jax.shard_map(
        functools.partial(body, mesh.shape["tm"], mesh.shape["env"]),
        mesh=mesh,
        in_specs=placed,
        out_specs=(P("tm", None, "env"), P(None, "env")),
        check_vma=False,
    )
```

time: 76.2 us -> 60.6 us (0.80)
  Pallas kernels: 67.3 us -> 57.6 us
  local copies, waits for them, and re-layouts: 7.69 us -> 2.17 us
    pallas_call x3 -> x1, Pallas kernels: 67.3 us -> 57.6 us  [body(): pl.pallas_call(functools.partial(kernel, tm, env, local, env_local * env)...]
    reshape x4 -> x0, local copies, waits for them, and re-layouts: 2.54 us -> none  [the longest x1 1.46 us: body(): m2 = mass_inverse.transpose(1, 0, 2).reshape(DOF, local * DOF)]
    unnamed x6 -> x4, local copies, waits for them, and re-layouts: 3.2 us -> 2.17 us
    transpose x1 -> x0, local copies, waits for them, and re-layouts: 0.83 us -> none  [body(): flat = jnp.concatenate([torque.reshape(steps * DOF, env_local), contact.a...]
where the time goes in v1:
time: 60.6 us; the launch traced here: 60.5 us
  Pallas kernels  57.6 us (95%)
  local copies, waits for them, and re-layouts  2.17 us (4%)
  between operations  0.65 us (1%)
    pallas_call x1, Pallas kernels, body(): pl.pallas_call(functools.partial(kernel, tm, env, local, env_local * env)...  57.6 us
    unnamed x4, local copies, waits for them, and re-layouts  2.17 us

profile of v1, /device:TPU:0, one launch (start us, length us, event | category | flops | bytes accessed | tf_op | source)
XLA Modules:
  0.0 60.5 jit_solution(9947507553035602858)
XLA Ops:
  0.6 57.6 %parareal.1 = (f32[70,2,256]{2,1,0:T(2,128)}, f32[3,256]{1,0:T(4,128)}) custom-call(f32[70,256]{1,0:T(8,128)} %init.1, f32[35,4,256]{2,1,0:T(4,128)} %bitcast.9, s32[4,256]{1,0:T(4,128)} %contact.1, f32[35,2,35]{2,1,0:T(2,128)} %bitcast.10, f32[1,35]{1,0:T(1,128)} %bitcast.11, f32[1,35]{1,0:T(1,128)} %bitcast.12, f32[1,35]{1,0:T(1,128)} %bitcast.13, ...), custom_call_target="tpu_custom_call" | custom-call | tf_op jit(solution)/shard_map/parareal/pallas_call | solution.py:426
  58.3 0.0 copy-start
  58.3 1.6 %copy.13 = f32[2,70,256]{2,0,1:T(2,128)} copy(f32[2,70,256]{2,0,1:T(2,128)} %bitcast.8) | data formatting | bytes 286720
  59.9 0.0 copy-done
  59.9 0.6 copy.14
Async XLA Ops:
  58.3 1.6 %copy-start = (f32[3,256]{1,0:T(4,128)S(1)}, f32[3,256]{1,0:T(4,128)}, u32[]{:S(2)}) copy-start(f32[3,256]{1,0:T(4,128)} %get-tuple-element.9) | copy-start | bytes 9220

commit v2 on v1

--- a/solution.py
+++ b/solution.py
@@ -27,8 +27,8 @@
 BF16 = jnp.bfloat16
 
 SIN = (
-    6.283182818551188, -41.341421398631915, 81.59618387021051,
-    -76.58010048603072, 41.205394649903326, -12.271261959178284,
+    6.2831825127387075, -41.34139305306742, 81.59546378559027,
+    -76.5727543587307, 41.17302274271854, -12.2199194670916,
 )
 
 
@@ -48,17 +48,45 @@
 class Plan:
     def __init__(self, slices):
         per = PER
+        order = list(range(1, slices)) + [0]
         self.groups = []
-        self.where = []
-        base = 0
+        self.where = {}
         for first in range(0, slices, per):
-            count = min(per, slices - first)
-            width = -(-count * DOF // LANES) * LANES
-            self.groups.append((base, width, first, count))
-            for pos in range(count):
-                self.where.append(base + pos * DOF)
-            base += width
-        self.lanes = base
+            members = order[first : first + per]
+            base = LANES * len(self.groups)
+            self.groups.append((base, members))
+            for pos, n in enumerate(members):
+                self.where[n] = base + pos * DOF
+        self.lanes = LANES * len(self.groups)
+        self.later = [g for g, (base, members) in enumerate(self.groups) if members != [0]]
+
+
+class Maps:
+    def __init__(self, slices):
+        self.index = {(n, n): n for n in range(slices)}
+        self.stage = {}
+        steps = {}
+
+        def need(first, last):
+            if (first, last) in steps or first == last:
+                return
+            half = 1 << ((last - first).bit_length() - 1)
+            need(first, first + half - 1)
+            need(first + half, last)
+            steps[first, last] = (half, (first, first + half - 1), (first + half, last))
+
+        half = 1
+        while half < slices:
+            self.stage[half] = []
+            for first in range(half, slices, 2 * half):
+                for n in range(first, min(first + half, slices)):
+                    need(first, n)
+            half *= 2
+        for key in steps:
+            self.index[key] = len(self.index)
+        for key, (half, left, right) in steps.items():
+            self.stage[half].append((self.index[key], self.index[left], self.index[right]))
+        self.count = len(self.index)
 
 
 class Message:
@@ -85,17 +113,19 @@
 
 def kernel(
     tm, env, local, total_env,
-    init, torque, contact, minv, stiff_r, damp_r, gravity_r, cstiff_r, cdamp_r,
+    contact_h, torque_h, minv_h, init_h, stiff_h, damp_h, gravity_h, cstiff_h, cdamp_h,
     states_out, corr_out,
+    contact, torque, minv, init, stiff_r, damp_r, gravity_r, cstiff_r, cdamp_r,
     tx, rx, row, rows, srow, sums, otx, orx, turn, mtile, own,
-    tq, spring, fric, grav, cspring, cfric, wgt, wtmp, ybuf, ubuf, by, bu, ly, lu, cmap, pmap, ctmp, xs,
-    tsend, trecv, esend, erecv, ssend, srecv, osend, orecv,
+    tq, spring, fric, grav, cspring, cfric, wgt, wtmp, ybuf, ubuf, by, bu, ly, lu, hmap, lmap, xs,
+    tsend, trecv, esend, erecv, ssend, srecv, osend, orecv, isem,
 ):
     slices = local * tm
     steps = local * HS
     env_local = contact.shape[1]
     epd = env_local // tm
     plan = Plan(slices)
+    maps = Maps(slices)
     msg = Message(steps, local, epd)
     me_t = lax.axis_index("tm")
     me_e = lax.axis_index("env")
@@ -111,6 +141,17 @@
         pl.semaphore_signal(barrier, inc=1, device_id=env_peer(k), device_id_type=MESH)
     for k in range(1, tm):
         pl.semaphore_signal(barrier, inc=1, device_id=tm_peer(k), device_id_type=MESH)
+
+    pairs = (
+        (contact_h, contact), (torque_h, torque), (minv_h, minv), (init_h, init),
+        (stiff_h, stiff_r), (damp_h, damp_r), (gravity_h, gravity_r),
+        (cstiff_h, cstiff_r), (cdamp_h, cdamp_r),
+    )
+    loads = [pltpu.make_async_copy(a, b, isem.at[i]) for i, (a, b) in enumerate(pairs)]
+    for c in loads:
+        c.start()
+    for c in loads:
+        c.wait()
 
     hits = contact[...].astype(F32)
     row[...] = jnp.zeros(row.shape, F32)
@@ -179,14 +220,12 @@
     stiff, damp, gravity, cstiff, cdamp = (
         r[...] for r in (stiff_r, damp_r, gravity_r, cstiff_r, cdamp_r))
     ratio = float(SUB)
-    block = 4 if slices % 4 == 0 else 1
-    unroll = max(1, min(SUB, 96 // len(plan.groups)))
+    unroll = SUB - 1 if len(plan.groups) * SUB <= 256 else 1
     to_u = TWO_PI / fine_dt
     for ref in (tq, spring, fric, grav, cspring, cfric, ybuf, ubuf, ly, lu):
         ref[...] = jnp.zeros(ref.shape, ref.dtype)
-    ctmp[...] = jnp.zeros(ctmp.shape, F32)
-    xs[...] = jnp.zeros(xs.shape, F32)
-    cmap[...] = jnp.zeros(cmap.shape, BF16)
+    for ref in (hmap, lmap):
+        ref[:, DEPTH:, :] = jnp.zeros((maps.count, LANES - DEPTH, LANES), BF16)
     rank = lax.broadcasted_iota(jnp.int32, (DEPTH, DOF), 0)
     col = lax.broadcasted_iota(jnp.int32, (DEPTH, DOF), 1)
     for n in range(slices):
@@ -215,19 +254,17 @@
             spring[j, :, cut] = TWO_PI * (stiff + hit * cstiff)
             fric[j, :, cut] = to_u * (damp + hit * cdamp)
 
-    for g, (base, width, first, count) in enumerate(plan.groups):
+    for g, (base, members) in enumerate(plan.groups):
         wtmp[...] = jnp.zeros(wtmp.shape, F32)
-        for pos in range(count):
-            src, here = divmod(first + pos, local)
+        for pos, n in enumerate(members):
+            src, here = divmod(n, local)
             start, lane = msg.place(steps + here)
             wtmp[pl.ds(pos * DOF, DOF), pl.ds(pos * DOF, DOF)] = (
                 fine_dt * fine_dt / TWO_PI
             ) * rx[src, start : start + DOF, lane : lane + DOF]
         high, low = split(wtmp[...])
-        wgt[g, 0:LANES, 0:LANES] = high
-        wgt[g, LANES:, 0:LANES] = high
-        wgt[g, 0:LANES, LANES:] = low
-        wgt[g, LANES:, LANES:] = jnp.zeros_like(low)
+        wgt[g, 0:LANES, :] = high
+        wgt[g, LANES:, :] = low
 
     for c in sum_copies:
         c.wait()
@@ -240,138 +277,135 @@
             cspring[j, :, cut] = TWO_PI * (stiff + gravity + mean * cstiff)
             cfric[j, :, cut] = to_u * (damp + mean * cdamp)
 
+    def once(part, g):
+        return dot(jnp.concatenate([part, part], axis=1), wgt[g])
+
     def product(force, g):
         high, low = split(force)
-        both = dot(jnp.concatenate([high, low], axis=1), wgt[g])
-        return both[:, :LANES] + both[:, LANES:]
-
-    for g, (base, width, first, count) in enumerate(plan.groups):
-        cut = pl.ds(base, width)
+        return once(high, g) + once(low, g)
+
+    lane_of = lax.broadcasted_iota(jnp.int32, (1, LANES), 1)
+    scale = jnp.where(lane_of < VOFF, TWO_PI, to_u)
+    shrink = jnp.where(lane_of < VOFF, 1.0 / TWO_PI, 1.0 / to_u)
+
+    def joined(y, u, depth):
+        gap = jnp.zeros((depth, VOFF - DOF), F32)
+        return jnp.concatenate(
+            [y, gap, u, jnp.zeros((depth, LANES - VOFF - DOF), F32)], axis=1)
+
+    def keep(index, value):
+        high, low = split(value)
+        hmap[index, 0:DEPTH, :] = high
+        lmap[index, 0:DEPTH, :] = low
+
+    def apply(high, low, index):
+        weight = hmap[index]
+        return dot(jnp.concatenate([high, low], axis=1),
+                   jnp.concatenate([weight, weight], axis=0)) + dot(high, lmap[index])
+
+    start = own[me_t] * shrink
+    xs[0] = start
+    ybuf[:, pl.ds(plan.where[0], DOF)] = start[:, 0:DOF]
+    ubuf[:, pl.ds(plan.where[0], DOF)] = start[:, VOFF : VOFF + DOF]
+    for g, (base, members) in enumerate(plan.groups):
+        cut = pl.ds(base, LANES)
         y, u = ly[:, cut], lu[:, cut]
+        b, a = ybuf[:, cut], ubuf[:, cut]
         for j in range(HS):
             force = -cspring[j, :, cut] * y - cfric[j, :, cut] * u
             u = u + ratio * product(force, g)
             y = y + ratio * u
+            force = tq[j, :, cut] - cspring[j, :, cut] * b - cfric[j, :, cut] * a
+            a = a + ratio * product(force, g)
+            b = b + ratio * a
         ly[:, cut] = y
         lu[:, cut] = u
-        u = ratio * product(tq[0, :, cut], g)
-        y = ratio * u
-        for j in range(1, HS):
-            force = tq[j, :, cut] - cspring[j, :, cut] * y - cfric[j, :, cut] * u
-            u = u + ratio * product(force, g)
-            y = y + ratio * u
-        by[:, cut] = y
-        bu[:, cut] = u
+        by[:, cut] = b
+        bu[:, cut] = a
     for n in range(slices):
         cut = pl.ds(plan.where[n], DOF)
-        ctmp[0:DEPTH, 0:DOF] = ly[:, cut]
-        ctmp[0:DEPTH, VOFF : VOFF + DOF] = lu[:, cut]
-        high, low = split(ctmp[...])
-        cmap[n, 0:LANES, 0:LANES] = high
-        cmap[n, LANES:, 0:LANES] = high
-        cmap[n, 0:LANES, LANES:] = low
-
-    def through(state, weight):
-        high, low = split(state)
-        both = dot(jnp.concatenate([high, low], axis=1), weight)
-        return both[:, :LANES] + both[:, LANES:]
-
-    def joined(y, u, depth):
-        gap = jnp.zeros((depth, VOFF - DOF), F32)
-        return jnp.concatenate(
-            [y, gap, u, jnp.zeros((depth, LANES - VOFF - DOF), F32)], axis=1)
-
-    firsts = range(0, slices, block)
-    running = {m: joined(ly[:, pl.ds(plan.where[m], DOF)], lu[:, pl.ds(plan.where[m], DOF)], DEPTH)
-               for m in firsts}
-    for i in range(1, block):
-        for m in firsts:
-            running[m] = through(running[m], cmap[m + i])
-            ctmp[0:DEPTH, :] = running[m]
-            high, low = split(ctmp[...])
-            pmap[m + i, 0:LANES, 0:LANES] = high
-            pmap[m + i, LANES:, 0:LANES] = high
-            pmap[m + i, 0:LANES, LANES:] = low
-            pmap[m + i, LANES:, LANES:] = jnp.zeros_like(low)
-
-    def sweep(offsets, entry):
-        ends = list(offsets)
-        for i in range(1, block):
-            for m in firsts:
-                ends[m + i] = through(ends[m + i - 1], cmap[m + i]) + ends[m + i]
-        enter = {}
-        for m in firsts:
-            enter[m] = entry
-            last = m + block - 1
-            whole = pmap if block > 1 else cmap
-            if entry is not None:
-                ends[last] = ends[last] + through(entry, whole[last])
-            entry = ends[last]
-        for i in range(block - 1):
-            for m in firsts:
-                if enter[m] is not None:
-                    part = cmap if i == 0 else pmap
-                    ends[m + i] = ends[m + i] + through(enter[m], part[m + i])
+        keep(n, joined(ly[:, cut], lu[:, cut], DEPTH))
+
+    def sweep(ends, compose=False):
+        ends = list(ends)
+        half = 1
+        while half < slices:
+            for first in range(half, slices, 2 * half):
+                high, low = split(ends[first - 1])
+                for n in range(min(first + half, slices) - 1, first - 1, -1):
+                    ends[n] = ends[n] + apply(high, low, maps.index[first, n])
+            if compose:
+                for target, left, right in maps.stage[half]:
+                    keep(target, apply(hmap[left, 0:DEPTH, :], lmap[left, 0:DEPTH, :], right))
+            half *= 2
         return ends
 
     def packed(yref, uref, n):
         cut = pl.ds(plan.where[n], DOF)
         return joined(yref[:, cut], uref[:, cut], epd)
 
-    lane_of = lax.broadcasted_iota(jnp.int32, (1, LANES), 1)
-    scale = jnp.where(lane_of < VOFF, TWO_PI, to_u)
-    shrink = jnp.where(lane_of < VOFF, 1.0 / TWO_PI, 1.0 / to_u)
-    state = own[me_t] * shrink
-    xs[0] = state
-    ends = sweep([packed(by, bu, n) for n in range(slices)], state)
+    ends = sweep([packed(by, bu, n) for n in range(slices)], True)
     for n in range(slices):
         xs[n + 1] = ends[n]
 
-    def iteration(k, corrections):
-        for n in range(slices):
+    def iteration(k, corrections, active, sliced):
+        for n in sliced:
             cut = pl.ds(plan.where[n], DOF)
             ybuf[:, cut] = xs[n, :, 0:DOF]
             ubuf[:, cut] = xs[n, :, VOFF : VOFF + DOF]
-        for j in range(HS):
-
-            def substep(counter, carry):
+        carry = []
+        for g in active:
+            cut = pl.ds(plan.groups[g][0], LANES)
+            y = ybuf[:, cut]
+            carry.append((y, ubuf[:, cut], y - jnp.round(y), jnp.zeros_like(y)))
+        carry = tuple(carry)
+
+        def horizon(j, carry):
+            def substep(flush, counter, carry):
                 result = []
-                for g, (base, width, first, count) in enumerate(plan.groups):
-                    y, u = carry[g]
-                    cut = pl.ds(base, width)
-                    t = y - jnp.round(y)
+                for g, (y, u, t, rest) in zip(active, carry):
+                    cut = pl.ds(plan.groups[g][0], LANES)
+                    ahead = y + u
+                    base = ahead - jnp.round(ahead)
                     s = t * t
-                    poly = jnp.full_like(s, SIN[-1])
-                    for c in SIN[-2::-1]:
-                        poly = poly * s + c
-                    force = (
-                        tq[j, :, cut]
-                        - spring[j, :, cut] * y
-                        - fric[j, :, cut] * u
-                        - (grav[:, cut] * t) * poly
-                    )
-                    u = u + product(force, g)
-                    y = y + u
-                    result.append((y, u))
+                    s2 = s * s
+                    poly = (SIN[5] * s + SIN[4]) * s2 + (SIN[3] * s + SIN[2])
+                    poly = poly * s2 + (SIN[1] * s + SIN[0])
+                    linear = ((tq[j, :, cut] + rest) - spring[j, :, cut] * y) - fric[j, :, cut] * u
+                    force = linear - (grav[:, cut] * t) * poly
+                    sent = force.astype(BF16)
+                    rest = force - sent.astype(F32)
+                    push = once(sent, g)
+                    if flush:
+                        push = push + once(rest.astype(BF16), g)
+                        rest = jnp.zeros_like(rest)
+                    result.append((ahead + push, u + push, base + push, rest))
                 return tuple(result)
 
-            first_state = tuple(
-                (ybuf[:, pl.ds(base, width)], ubuf[:, pl.ds(base, width)])
-                for base, width, first, count in plan.groups
-            )
-            last = lax.fori_loop(0, SUB, substep, first_state, unroll=unroll)
-            for g, (base, width, first, count) in enumerate(plan.groups):
-                ybuf[:, pl.ds(base, width)] = last[g][0]
-                ubuf[:, pl.ds(base, width)] = last[g][1]
+            carry = lax.fori_loop(0, SUB - 1, functools.partial(substep, False), carry, unroll=unroll)
+            return substep(True, SUB - 1, carry)
+
+        carry = lax.fori_loop(0, HS, horizon, carry)
+        for g, (y, u, t, rest) in zip(active, carry):
+            cut = pl.ds(plan.groups[g][0], LANES)
+            ybuf[:, cut] = y
+            ubuf[:, cut] = u
         worst = jnp.zeros((epd, 1), F32)
-        changes = sweep([packed(ybuf, ubuf, n) - xs[n + 1] for n in range(slices)], None)
+        moved = [packed(ybuf, ubuf, n) - xs[n + 1] if n in sliced else None for n in range(slices)]
+        if moved[0] is None:
+            moved[0] = jnp.zeros((epd, LANES), F32)
+        changes = sweep(moved, None)
         for n in range(slices):
             real = changes[n] * scale
             worst = jnp.maximum(worst, jnp.sum(real * real, axis=1, keepdims=True))
             xs[n + 1] = xs[n + 1] + changes[n]
         return jnp.where(lane_of == DOF + k, jnp.sqrt(worst), corrections)
 
-    corrections = lax.fori_loop(0, ITERS, iteration, jnp.zeros((epd, LANES), F32))
+    groups = range(len(plan.groups))
+    corrections = iteration(0, jnp.zeros((epd, LANES), F32), groups, range(slices))
+    live = [n for g in plan.later for n in plan.groups[g][1]]
+    corrections = lax.fori_loop(
+        1, ITERS, lambda k, kept: iteration(k, kept, plan.later, live), corrections)
 
     span = local * epd
     for t in range(tm):
@@ -413,6 +447,7 @@
     steps = local * HS
     slices = local * tm
     plan = Plan(slices)
+    maps = Maps(slices).count
     msg = Message(steps, local, epd)
     vmem = pl.BlockSpec(memory_space=pltpu.VMEM)
     dma = pltpu.SemaphoreType.DMA
@@ -426,12 +461,17 @@
     states, corrections = pl.pallas_call(
         functools.partial(kernel, tm, env, local, env_local * env),
         out_shape=(
-            jax.ShapeDtypeStruct((2 * DOF, local, env_local), F32),
-            jax.ShapeDtypeStruct((ITERS, env_local), F32),
+            pltpu.VMEM((2 * DOF, local, env_local), F32),
+            pltpu.VMEM((ITERS, env_local), F32),
         ),
-        in_specs=[vmem] * 9,
+        in_specs=[pl.BlockSpec(memory_space=pl.ANY)] * 9,
         out_specs=(vmem, vmem),
         scratch_shapes=[
+            pltpu.VMEM((steps, env_local), jnp.int32),
+            pltpu.VMEM((DOF, steps, env_local), F32),
+            pltpu.VMEM((DOF, local, DOF), F32),
+            pltpu.VMEM((2 * DOF, env_local), F32),
+        ] + [pltpu.VMEM((1, DOF), F32)] * 5 + [
             pltpu.VMEM((tm, msg.total, LANES), F32), pltpu.VMEM((tm, msg.total, LANES), F32),
             pltpu.VMEM(row, F32), pltpu.VMEM((env,) + row, F32),
             pltpu.VMEM(row, F32), pltpu.VMEM((tm,) + row, F32),
@@ -440,21 +480,19 @@
             pltpu.VMEM((max(msg.rows), LANES), F32),
             pltpu.VMEM((tm, epd, LANES), F32),
             both, both, both, pltpu.VMEM((1, lanes), F32), thin, thin,
-            pltpu.VMEM((groups, WIDE, WIDE), BF16),
+            pltpu.VMEM((groups, WIDE, LANES), BF16),
             pltpu.VMEM((LANES, LANES), F32),
             big, big, big, big,
             pltpu.VMEM((DEPTH, lanes), F32), pltpu.VMEM((DEPTH, lanes), F32),
-            pltpu.VMEM((slices, 2 * LANES, 2 * LANES), BF16),
-            pltpu.VMEM((slices, 2 * LANES, 2 * LANES), BF16),
-            pltpu.VMEM((LANES, LANES), F32),
+            pltpu.VMEM((maps, LANES, LANES), BF16), pltpu.VMEM((maps, LANES, LANES), BF16),
             pltpu.VMEM((slices + 1, epd, LANES), F32),
             dma((tm,)), dma((tm,)), dma((env,)), dma((env,)),
-            dma((tm,)), dma((tm,)), dma((tm,)), dma((tm,)),
+            dma((tm,)), dma((tm,)), dma((tm,)), dma((tm,)), dma((9,)),
         ],
         compiler_params=pltpu.CompilerParams(collective_id=0, has_side_effects=True),
         name="parareal",
-    )(init_state, jnp.transpose(torque, (1, 0, 2)), contact,
-      jnp.transpose(mass_inverse, (1, 0, 2)), *prm)
+    )(contact, jnp.transpose(torque, (1, 0, 2)),
+      jnp.transpose(mass_inverse, (1, 0, 2)), init_state, *prm)
     return jnp.transpose(states, (1, 0, 2)), corrections
 
 

time: 60.6 us -> 56.5 us (0.932)
  Pallas kernels: 57.6 us -> 54.4 us
  local copies, waits for them, and re-layouts: 2.17 us -> 1.25 us
    pallas_call x1, Pallas kernels: 57.6 us -> 54.4 us  [body(): pl.pallas_call(functools.partial(kernel, tm, env, local, env_local * env)...]
    unnamed x4 -> x2, local copies, waits for them, and re-layouts: 2.17 us -> 1.25 us
where the time goes in v2:
time: 56.5 us; the launch traced here: 56.3 us
  Pallas kernels  54.4 us (96%)
  local copies, waits for them, and re-layouts  1.25 us (2%)
  between operations  0.64 us (1%)
    pallas_call x1, Pallas kernels, body(): pl.pallas_call(functools.partial(kernel, tm, env, local, env_local * env)...  54.4 us
    unnamed x2, local copies, waits for them, and re-layouts  1.25 us

profile of v2, /device:TPU:0, one launch (start us, length us, event | category | flops | bytes accessed | tf_op | source)
XLA Modules:
  0.0 56.3 jit_solution(17500664146316728110)
XLA Ops:
  0.6 54.4 %parareal.1 = (f32[70,2,256]{2,1,0:T(2,128)S(1)}, f32[3,256]{1,0:T(4,128)S(1)}) custom-call(s32[4,256]{1,0:T(4,128)} %contact_h.1, f32[35,4,256]{2,1,0:T(4,128)} %bitcast.9, f32[35,2,35]{2,1,0:T(2,128)} %bitcast.10, f32[70,256]{1,0:T(8,128)} %init_h.1, f32[1,35]{1,0:T(1,128)} %bitcast.11, f32[1,35]{1,0:T(1,128)} %bitcast.12, f32[1,35]{1,0:T(1,128)} %bitcast.13, ...), custom_call_target="tpu_custom_call" | custom-call | tf_op jit(solution)/shard_map/parareal/pallas_call | solution.py:461
  55.0 0.7 %copy.13 = f32[2,70,256]{2,0,1:T(2,128)} copy(f32[2,70,256]{2,0,1:T(2,128)S(1)} %bitcast.8) | data formatting | bytes 286720
  55.7 0.6 %copy.14 = f32[3,256]{1,0:T(4,128)} copy(f32[3,256]{1,0:T(4,128)S(1)} %get-tuple-element.7) | data formatting | bytes 6144

commit v3 on v2

--- a/solution.py
+++ b/solution.py
@@ -117,8 +117,8 @@
     states_out, corr_out,
     contact, torque, minv, init, stiff_r, damp_r, gravity_r, cstiff_r, cdamp_r,
     tx, rx, row, rows, srow, sums, otx, orx, turn, mtile, own,
-    tq, spring, fric, grav, cspring, cfric, wgt, wtmp, ybuf, ubuf, by, bu, ly, lu, hmap, lmap, xs,
-    tsend, trecv, esend, erecv, ssend, srecv, osend, orecv, isem,
+    tq, spring, fric, prow, cspring, cfric, wgt, wtmp, ybuf, ubuf, by, bu, ly, lu, maps_w, xs,
+    tsem, esem, ssem, osem, isem,
 ):
     slices = local * tm
     steps = local * HS
@@ -150,12 +150,13 @@
     loads = [pltpu.make_async_copy(a, b, isem.at[i]) for i, (a, b) in enumerate(pairs)]
     for c in loads:
         c.start()
-    for c in loads:
-        c.wait()
-
+    loads[0].wait()
     hits = contact[...].astype(F32)
     row[...] = jnp.zeros(row.shape, F32)
     row[0:steps, :] = jnp.broadcast_to(jnp.sum(hits, axis=1, keepdims=True), (steps, LANES))
+    for c in loads[1:3]:
+        c.wait()
+
     for tile in range(msg.tiles):
         turn[...] = jnp.zeros(turn.shape, F32)
         mtile[...] = jnp.zeros(mtile.shape, F32)
@@ -178,104 +179,124 @@
                 tx[p, first : first + epd, :] = tx[p, first : first + epd, :] + chunk
             else:
                 tx[p, first : first + epd, :] = chunk
+
+    pl.semaphore_wait(barrier, tm + env - 2)
+
+    def sends(src, dst, sem, count, peer):
+        return [
+            pltpu.make_async_remote_copy(
+                src_ref=src(k), dst_ref=dst, send_sem=sem.at[0], recv_sem=sem.at[1],
+                device_id=peer(k), device_id_type=MESH)
+            for k in range(1, count)
+        ]
+
+    def finish(src, dst, sem, peer):
+        all_of = pltpu.make_async_remote_copy(
+            src_ref=src, dst_ref=dst, send_sem=sem.at[0], recv_sem=sem.at[1],
+            device_id=peer(1), device_id_type=MESH)
+        all_of.wait_send()
+        all_of.wait_recv()
+
+    def to_peer(ref):
+        return lambda k: ref.at[lax.rem(me_t + k, tm)]
+
+    most, few = pl.ds(0, tm - 1), pl.ds(0, env - 1)
+    for c in sends(lambda k: row, rows.at[me_e], esem, env, env_peer):
+        c.start()
+    for c in sends(to_peer(tx), rx.at[me_t], tsem, tm, tm_peer):
+        c.start()
+    for c in loads[3:]:
+        c.wait()
     turn[...] = jnp.zeros(turn.shape, F32)
     turn[0:DOF, :] = init[0:DOF, :]
     turn[VOFF : VOFF + DOF, :] = init[DOF : 2 * DOF, :]
     turned = turn[...].T
     for p in range(tm):
         own[p] = turned[p * epd : (p + 1) * epd]
-
-    pl.semaphore_wait(barrier, tm + env - 2)
-
-    def row_copy(k):
-        return pltpu.make_async_remote_copy(
-            src_ref=row, dst_ref=rows.at[me_e], send_sem=esend.at[k], recv_sem=erecv.at[k],
-            device_id=env_peer(k), device_id_type=MESH)
-
-    def block_copy(k):
-        return pltpu.make_async_remote_copy(
-            src_ref=tx.at[lax.rem(me_t + k, tm)], dst_ref=rx.at[me_t],
-            send_sem=tsend.at[k], recv_sem=trecv.at[k],
-            device_id=tm_peer(k), device_id_type=MESH)
-
-    def sum_copy(k):
-        return pltpu.make_async_remote_copy(
-            src_ref=srow, dst_ref=sums.at[me_t], send_sem=ssend.at[k], recv_sem=srecv.at[k],
-            device_id=tm_peer(k), device_id_type=MESH)
-
-    def out_copy(k):
-        return pltpu.make_async_remote_copy(
-            src_ref=otx.at[lax.rem(me_t + k, tm)], dst_ref=orx.at[me_t],
-            send_sem=osend.at[k], recv_sem=orecv.at[k],
-            device_id=tm_peer(k), device_id_type=MESH)
-
-    row_copies = [row_copy(k) for k in range(1, env)]
-    block_copies = [block_copy(k) for k in range(1, tm)]
-    sum_copies = [sum_copy(k) for k in range(1, tm)]
-    for c in row_copies + block_copies:
-        c.start()
     rows[me_e] = row[...]
     rx[me_t] = tx[me_t]
 
-    stiff, damp, gravity, cstiff, cdamp = (
-        r[...] for r in (stiff_r, damp_r, gravity_r, cstiff_r, cdamp_r))
     ratio = float(SUB)
-    unroll = SUB - 1 if len(plan.groups) * SUB <= 256 else 1
     to_u = TWO_PI / fine_dt
-    for ref in (tq, spring, fric, grav, cspring, cfric, ybuf, ubuf, ly, lu):
+    high_rows = up8(epd)
+    lane_of = lax.broadcasted_iota(jnp.int32, (1, LANES), 1)
+    wide_lane = lax.broadcasted_iota(jnp.int32, (high_rows, LANES), 1)
+
+    prow[...] = jnp.zeros(prow.shape, F32)
+    for i, ref in enumerate((stiff_r, damp_r, gravity_r, cstiff_r, cdamp_r)):
+        for pos in range(PER):
+            prow[i : i + 1, pos * DOF : (pos + 1) * DOF] = ref[...]
+    stiff, damp, gravity, cstiff, cdamp = (prow[i : i + 1, :] for i in range(5))
+    for ref in (ybuf, ubuf, ly, lu):
         ref[...] = jnp.zeros(ref.shape, ref.dtype)
-    for ref in (hmap, lmap):
-        ref[:, DEPTH:, :] = jnp.zeros((maps.count, LANES - DEPTH, LANES), BF16)
+    maps_w[:, 3 * DEPTH :, :] = jnp.zeros((maps.count, WIDE - 3 * DEPTH, LANES), BF16)
     rank = lax.broadcasted_iota(jnp.int32, (DEPTH, DOF), 0)
     col = lax.broadcasted_iota(jnp.int32, (DEPTH, DOF), 1)
     for n in range(slices):
-        cut = pl.ds(plan.where[n], DOF)
-        grav[:, cut] = gravity
-        ly[:, cut] = jnp.where(rank == col, 1.0, 0.0)
-        lu[:, cut] = jnp.where(rank == col + VOFF, 1.0, 0.0)
-
-    for c in row_copies:
-        c.wait()
+        span_n = pl.ds(plan.where[n], DOF)
+        ly[:, span_n] = jnp.where(rank == col, 1.0, 0.0)
+        lu[:, span_n] = jnp.where(rank == col + VOFF, 1.0, 0.0)
+
+    finish(rows.at[few], rows.at[few], esem, env_peer)
     srow[...] = jnp.sum(rows[...], axis=0) * (1.0 / total_env)
-    for c in sum_copies:
+    for c in sends(lambda k: srow, sums.at[me_t], ssem, tm, tm_peer):
         c.start()
     sums[me_t] = srow[...]
-    for c in block_copies:
-        c.wait()
-
-    for n in range(slices):
-        src, pos = divmod(n, local)
-        cut = pl.ds(plan.where[n], DOF)
+    finish(tx.at[most], rx.at[most], tsem, tm_peer)
+
+    def by_lane(values, lanes):
+        out = values[0]
+        for pos in range(1, len(values)):
+            out = jnp.where(lanes >= pos * DOF, values[pos], out)
+        return out
+
+    def moved_to(value, shift):
+        shift = shift % LANES
+        return pltpu.roll(value, shift, 1) if shift else value
+
+    for g, (base, members) in enumerate(plan.groups):
+        span_g = pl.ds(base, LANES)
         for j in range(HS):
-            step = pos * HS + j
-            first, lane = msg.place(step)
-            hit = rx[src, 0:epd, SPARE + step : SPARE + step + 1]
-            tq[j, :, cut] = rx[src, first : first + epd, lane : lane + DOF]
-            spring[j, :, cut] = TWO_PI * (stiff + hit * cstiff)
-            fric[j, :, cut] = to_u * (damp + hit * cdamp)
-
+            force, hit = [], []
+            for pos, n in enumerate(members):
+                src, here = divmod(n, local)
+                step = here * HS + j
+                first, lane = msg.place(step)
+                piece = rx[src, first : first + high_rows, :]
+                force.append(moved_to(piece, pos * DOF - lane))
+                flag = rx[src, 0:high_rows, SPARE + step : SPARE + step + 1]
+                hit.append(jnp.broadcast_to(flag, (high_rows, LANES)))
+            touch = by_lane(hit, wide_lane)[0:epd]
+            tq[j, :, span_g] = by_lane(force, wide_lane)[0:epd]
+            spring[j, :, span_g] = TWO_PI * stiff + touch * (TWO_PI * cstiff)
+            fric[j, :, span_g] = to_u * damp + touch * (to_u * cdamp)
+
+    tall_lane = lax.broadcasted_iota(jnp.int32, (VOFF, LANES), 1)
     for g, (base, members) in enumerate(plan.groups):
         wtmp[...] = jnp.zeros(wtmp.shape, F32)
         for pos, n in enumerate(members):
             src, here = divmod(n, local)
-            start, lane = msg.place(steps + here)
-            wtmp[pl.ds(pos * DOF, DOF), pl.ds(pos * DOF, DOF)] = (
-                fine_dt * fine_dt / TWO_PI
-            ) * rx[src, start : start + DOF, lane : lane + DOF]
+            first, lane = msg.place(steps + here)
+            piece = moved_to(rx[src, first : first + VOFF, :], pos * DOF - lane)
+            inside = (tall_lane >= pos * DOF) & (tall_lane < (pos + 1) * DOF)
+            piece = jnp.where(inside, (fine_dt * fine_dt / TWO_PI) * piece, 0.0)
+            wtmp[pl.ds(pos * DOF, DOF), :] = piece[0:DOF]
         high, low = split(wtmp[...])
         wgt[g, 0:LANES, :] = high
         wgt[g, LANES:, :] = low
 
-    for c in sum_copies:
-        c.wait()
-    for n in range(slices):
-        src, pos = divmod(n, local)
-        cut = pl.ds(plan.where[n], DOF)
+    finish(sums.at[most], sums.at[most], ssem, tm_peer)
+    for g, (base, members) in enumerate(plan.groups):
+        span_g = pl.ds(base, LANES)
         for j in range(HS):
-            step = pos * HS + j
-            mean = sums[src, step : step + 1, 0:DOF]
-            cspring[j, :, cut] = TWO_PI * (stiff + gravity + mean * cstiff)
-            cfric[j, :, cut] = to_u * (damp + mean * cdamp)
+            means = []
+            for n in members:
+                src, here = divmod(n, local)
+                step = here * HS + j
+                means.append(sums[src, step : step + 1, :])
+            mean = by_lane(means, lane_of)
+            cspring[j, :, span_g] = TWO_PI * (stiff + gravity + mean * cstiff)
+            cfric[j, :, span_g] = to_u * (damp + mean * cdamp)
 
     def once(part, g):
         return dot(jnp.concatenate([part, part], axis=1), wgt[g])
@@ -284,7 +305,6 @@
         high, low = split(force)
         return once(high, g) + once(low, g)
 
-    lane_of = lax.broadcasted_iota(jnp.int32, (1, LANES), 1)
     scale = jnp.where(lane_of < VOFF, TWO_PI, to_u)
     shrink = jnp.where(lane_of < VOFF, 1.0 / TWO_PI, 1.0 / to_u)
 
@@ -293,35 +313,49 @@
         return jnp.concatenate(
             [y, gap, u, jnp.zeros((depth, LANES - VOFF - DOF), F32)], axis=1)
 
+    spill = 2 * DEPTH - LANES
+
+    def spread(value):
+        lanes = lax.broadcasted_iota(jnp.int32, value.shape, 1)
+        high = value.astype(BF16).astype(F32)
+        low = moved_to(value - high, DEPTH)
+        left = jnp.where(lanes < DEPTH, high, low)
+        right = jnp.where(lanes < spill, low, moved_to(high, spill))
+        return jnp.concatenate([left, right], axis=1).astype(BF16)
+
+    values = {}
+
     def keep(index, value):
+        values[index] = value
         high, low = split(value)
-        hmap[index, 0:DEPTH, :] = high
-        lmap[index, 0:DEPTH, :] = low
-
-    def apply(high, low, index):
-        weight = hmap[index]
-        return dot(jnp.concatenate([high, low], axis=1),
-                   jnp.concatenate([weight, weight], axis=0)) + dot(high, lmap[index])
+        maps_w[index, 0:DEPTH, :] = high
+        maps_w[index, DEPTH : 2 * DEPTH, :] = high
+        maps_w[index, 2 * DEPTH : 3 * DEPTH, :] = low
+
+    def apply(left, index):
+        return dot(left, maps_w[index])
 
     start = own[me_t] * shrink
     xs[0] = start
     ybuf[:, pl.ds(plan.where[0], DOF)] = start[:, 0:DOF]
     ubuf[:, pl.ds(plan.where[0], DOF)] = start[:, VOFF : VOFF + DOF]
-    for g, (base, members) in enumerate(plan.groups):
-        cut = pl.ds(base, LANES)
-        y, u = ly[:, cut], lu[:, cut]
-        b, a = ybuf[:, cut], ubuf[:, cut]
-        for j in range(HS):
-            force = -cspring[j, :, cut] * y - cfric[j, :, cut] * u
-            u = u + ratio * product(force, g)
-            y = y + ratio * u
-            force = tq[j, :, cut] - cspring[j, :, cut] * b - cfric[j, :, cut] * a
-            a = a + ratio * product(force, g)
-            b = b + ratio * a
-        ly[:, cut] = y
-        lu[:, cut] = u
-        by[:, cut] = b
-        bu[:, cut] = a
+    spans = [pl.ds(base, LANES) for base, members in plan.groups]
+    every = range(len(spans))
+    y, u = [ly[:, c] for c in spans], [lu[:, c] for c in spans]
+    b, a = [ybuf[:, c] for c in spans], [ubuf[:, c] for c in spans]
+    for j in range(HS):
+        for g in every:
+            c = spans[g]
+            force = tq[j, :, c] - cspring[j, :, c] * b[g] - cfric[j, :, c] * a[g]
+            a[g] = a[g] + ratio * product(force, g)
+            force = -cspring[j, :, c] * y[g] - cfric[j, :, c] * u[g]
+            u[g] = u[g] + ratio * product(force, g)
+        for g in every:
+            b[g] = b[g] + ratio * a[g]
+            y[g] = y[g] + ratio * u[g]
+    for g in every:
+        ly[:, spans[g]], lu[:, spans[g]] = y[g], u[g]
+        by[:, spans[g]], bu[:, spans[g]] = b[g], a[g]
     for n in range(slices):
         cut = pl.ds(plan.where[n], DOF)
         keep(n, joined(ly[:, cut], lu[:, cut], DEPTH))
@@ -331,12 +365,12 @@
         half = 1
         while half < slices:
             for first in range(half, slices, 2 * half):
-                high, low = split(ends[first - 1])
+                left = spread(ends[first - 1])
                 for n in range(min(first + half, slices) - 1, first - 1, -1):
-                    ends[n] = ends[n] + apply(high, low, maps.index[first, n])
+                    ends[n] = ends[n] + apply(left, maps.index[first, n])
             if compose:
                 for target, left, right in maps.stage[half]:
-                    keep(target, apply(hmap[left, 0:DEPTH, :], lmap[left, 0:DEPTH, :], right))
+                    keep(target, apply(spread(values[left]), right))
             half *= 2
         return ends
 
@@ -347,6 +381,9 @@
     ends = sweep([packed(by, bu, n) for n in range(slices)], True)
     for n in range(slices):
         xs[n + 1] = ends[n]
+
+    unroll = SUB - 1 if len(plan.groups) * SUB <= 256 else 1
+    grav = gravity
 
     def iteration(k, corrections, active, sliced):
         for n in sliced:
@@ -369,10 +406,12 @@
                     base = ahead - jnp.round(ahead)
                     s = t * t
                     s2 = s * s
-                    poly = (SIN[5] * s + SIN[4]) * s2 + (SIN[3] * s + SIN[2])
-                    poly = poly * s2 + (SIN[1] * s + SIN[0])
+                    weight = grav * t
+                    weight2 = weight * s2
                     linear = ((tq[j, :, cut] + rest) - spring[j, :, cut] * y) - fric[j, :, cut] * u
-                    force = linear - (grav[:, cut] * t) * poly
+                    force = linear - weight * (SIN[1] * s + SIN[0])
+                    force = force - weight2 * (SIN[3] * s + SIN[2])
+                    force = force - (weight2 * s2) * (SIN[5] * s + SIN[4])
                     sent = force.astype(BF16)
                     rest = force - sent.astype(F32)
                     push = once(sent, g)
@@ -385,7 +424,11 @@
             carry = lax.fori_loop(0, SUB - 1, functools.partial(substep, False), carry, unroll=unroll)
             return substep(True, SUB - 1, carry)
 
-        carry = lax.fori_loop(0, HS, horizon, carry)
+        if unroll > 1:
+            for j in range(HS):
+                carry = horizon(j, carry)
+        else:
+            carry = lax.fori_loop(0, HS, horizon, carry)
         for g, (y, u, t, rest) in zip(active, carry):
             cut = pl.ds(plan.groups[g][0], LANES)
             ybuf[:, cut] = y
@@ -414,12 +457,10 @@
         turned = jnp.concatenate(parts, axis=0).T
         otx[t, :, 0:span] = turned[0:VOFF]
         otx[t, :, span : 2 * span] = turned[VOFF:DEPTH]
-    out_copies = [out_copy(k) for k in range(1, tm)]
-    for c in out_copies:
+    for c in sends(to_peer(otx), orx.at[me_t], osem, tm, tm_peer):
         c.start()
     orx[me_t] = otx[me_t]
-    for c in out_copies:
-        c.wait()
+    finish(otx.at[most], orx.at[most], osem, tm_peer)
 
     across = LANES // epd
     lanes = lax.broadcasted_iota(jnp.int32, (VOFF, LANES), 1)
@@ -479,15 +520,14 @@
             pltpu.VMEM((LANES, env_local), F32),
             pltpu.VMEM((max(msg.rows), LANES), F32),
             pltpu.VMEM((tm, epd, LANES), F32),
-            both, both, both, pltpu.VMEM((1, lanes), F32), thin, thin,
+            both, both, both, pltpu.VMEM((8, LANES), F32), thin, thin,
             pltpu.VMEM((groups, WIDE, LANES), BF16),
             pltpu.VMEM((LANES, LANES), F32),
             big, big, big, big,
             pltpu.VMEM((DEPTH, lanes), F32), pltpu.VMEM((DEPTH, lanes), F32),
-            pltpu.VMEM((maps, LANES, LANES), BF16), pltpu.VMEM((maps, LANES, LANES), BF16),
+            pltpu.VMEM((maps, WIDE, LANES), BF16),
             pltpu.VMEM((slices + 1, epd, LANES), F32),
-            dma((tm,)), dma((tm,)), dma((env,)), dma((env,)),
-            dma((tm,)), dma((tm,)), dma((tm,)), dma((tm,)), dma((9,)),
+            dma((2,)), dma((2,)), dma((2,)), dma((2,)), dma((9,)),
         ],
         compiler_params=pltpu.CompilerParams(collective_id=0, has_side_effects=True),
         name="parareal",

time: 56.5 us -> 52.7 us (0.933)
  Pallas kernels: 54.4 us -> 50.6 us
    pallas_call x1, Pallas kernels: 54.4 us -> 50.6 us  [body(): pl.pallas_call(functools.partial(kernel, tm, env, local, env_local * env)...]
where the time goes in v3:
time: 52.7 us; the launch traced here: 52.5 us
  Pallas kernels  50.6 us (96%)
  local copies, waits for them, and re-layouts  1.25 us (2%)
  between operations  0.64 us (1%)
    pallas_call x1, Pallas kernels, body(): pl.pallas_call(functools.partial(kernel, tm, env, local, env_local * env)...  50.6 us
    unnamed x2, local copies, waits for them, and re-layouts  1.25 us

profile of v3, /device:TPU:0, one launch (start us, length us, event | category | flops | bytes accessed | tf_op | source)
XLA Modules:
  0.0 52.5 jit_solution(4749831685728508035)
XLA Ops:
  0.6 50.6 %parareal.1 = (f32[70,2,256]{2,1,0:T(2,128)S(1)}, f32[3,256]{1,0:T(4,128)S(1)}) custom-call(s32[4,256]{1,0:T(4,128)} %contact_h.1, f32[35,4,256]{2,1,0:T(4,128)} %bitcast.9, f32[35,2,35]{2,1,0:T(2,128)} %bitcast.10, f32[70,256]{1,0:T(8,128)} %init_h.1, f32[1,35]{1,0:T(1,128)} %bitcast.11, f32[1,35]{1,0:T(1,128)} %bitcast.12, f32[1,35]{1,0:T(1,128)} %bitcast.13, ...), custom_call_target="tpu_custom_call" | custom-call | tf_op jit(solution)/shard_map/parareal/pallas_call | solution.py:502
  51.3 0.7 %copy.13 = f32[2,70,256]{2,0,1:T(2,128)} copy(f32[2,70,256]{2,0,1:T(2,128)S(1)} %bitcast.8) | data formatting | bytes 286720
  51.9 0.6 %copy.14 = f32[3,256]{1,0:T(4,128)} copy(f32[3,256]{1,0:T(4,128)S(1)} %get-tuple-element.7) | data formatting | bytes 6144

commit v4 on v3

--- a/solution.py
+++ b/solution.py
@@ -87,6 +87,10 @@
         for key, (half, left, right) in steps.items():
             self.stage[half].append((self.index[key], self.index[left], self.index[right]))
         self.count = len(self.index)
+        self.after = {
+            (half, right): (target, left)
+            for half, stage in self.stage.items() for target, left, right in stage
+        }
 
 
 class Message:
@@ -118,7 +122,7 @@
     contact, torque, minv, init, stiff_r, damp_r, gravity_r, cstiff_r, cdamp_r,
     tx, rx, row, rows, srow, sums, otx, orx, turn, mtile, own,
     tq, spring, fric, prow, cspring, cfric, wgt, wtmp, ybuf, ubuf, by, bu, ly, lu, maps_w, xs,
-    tsem, esem, ssem, osem, isem,
+    tsem, esem, ssem, osem, csem, isem, delta, corr_t, ctx, crx,
 ):
     slices = local * tm
     steps = local * HS
@@ -229,7 +233,9 @@
     stiff, damp, gravity, cstiff, cdamp = (prow[i : i + 1, :] for i in range(5))
     for ref in (ybuf, ubuf, ly, lu):
         ref[...] = jnp.zeros(ref.shape, ref.dtype)
-    maps_w[:, 3 * DEPTH :, :] = jnp.zeros((maps.count, WIDE - 3 * DEPTH, LANES), BF16)
+    for half in range(2):
+        tail = pl.ds(half * LANES + DEPTH, LANES - DEPTH)
+        maps_w[:, tail, :] = jnp.zeros((maps.count, LANES - DEPTH, LANES), BF16)
     rank = lax.broadcasted_iota(jnp.int32, (DEPTH, DOF), 0)
     col = lax.broadcasted_iota(jnp.int32, (DEPTH, DOF), 1)
     for n in range(slices):
@@ -254,6 +260,11 @@
         shift = shift % LANES
         return pltpu.roll(value, shift, 1) if shift else value
 
+    pick_row = lax.broadcasted_iota(jnp.int32, (LANES, steps * LANES), 0)
+    pick_col = lax.broadcasted_iota(jnp.int32, (LANES, steps * LANES), 1)
+    pick = jnp.where(pick_row == SPARE + pick_col // LANES, 1.0, 0.0).astype(BF16)
+    flags = dot(jnp.concatenate(
+        [rx[t, 0:high_rows, :] for t in range(tm)], axis=0).astype(BF16), pick)
     for g, (base, members) in enumerate(plan.groups):
         span_g = pl.ds(base, LANES)
         for j in range(HS):
@@ -264,8 +275,8 @@
                 first, lane = msg.place(step)
                 piece = rx[src, first : first + high_rows, :]
                 force.append(moved_to(piece, pos * DOF - lane))
-                flag = rx[src, 0:high_rows, SPARE + step : SPARE + step + 1]
-                hit.append(jnp.broadcast_to(flag, (high_rows, LANES)))
+                hit.append(flags[src * high_rows : (src + 1) * high_rows,
+                                 step * LANES : (step + 1) * LANES])
             touch = by_lane(hit, wide_lane)[0:epd]
             tq[j, :, span_g] = by_lane(force, wide_lane)[0:epd]
             spring[j, :, span_g] = TWO_PI * stiff + touch * (TWO_PI * cstiff)
@@ -303,7 +314,12 @@
 
     def product(force, g):
         high, low = split(force)
-        return once(high, g) + once(low, g)
+        top, rest = wgt[g, 0:LANES, :], wgt[g, LANES:, :]
+        weight = jnp.concatenate([
+            jnp.concatenate([top, rest], axis=1),
+            jnp.concatenate([top, jnp.zeros_like(rest)], axis=1)], axis=0)
+        both = dot(jnp.concatenate([high, low], axis=1), weight)
+        return both[:, :LANES] + both[:, LANES:]
 
     scale = jnp.where(lane_of < VOFF, TWO_PI, to_u)
     shrink = jnp.where(lane_of < VOFF, 1.0 / TWO_PI, 1.0 / to_u)
@@ -313,27 +329,18 @@
         return jnp.concatenate(
             [y, gap, u, jnp.zeros((depth, LANES - VOFF - DOF), F32)], axis=1)
 
-    spill = 2 * DEPTH - LANES
-
-    def spread(value):
-        lanes = lax.broadcasted_iota(jnp.int32, value.shape, 1)
-        high = value.astype(BF16).astype(F32)
-        low = moved_to(value - high, DEPTH)
-        left = jnp.where(lanes < DEPTH, high, low)
-        right = jnp.where(lanes < spill, low, moved_to(high, spill))
-        return jnp.concatenate([left, right], axis=1).astype(BF16)
-
     values = {}
 
     def keep(index, value):
         values[index] = value
         high, low = split(value)
         maps_w[index, 0:DEPTH, :] = high
-        maps_w[index, DEPTH : 2 * DEPTH, :] = high
-        maps_w[index, 2 * DEPTH : 3 * DEPTH, :] = low
-
-    def apply(left, index):
-        return dot(left, maps_w[index])
+        maps_w[index, LANES : LANES + DEPTH, :] = low
+
+    def apply(high, low, index):
+        weight = maps_w[index, 0:LANES, :]
+        return dot(jnp.concatenate([high, low], axis=1),
+                   jnp.concatenate([weight, weight], axis=0)) + dot(high, maps_w[index, LANES:, :])
 
     start = own[me_t] * shrink
     xs[0] = start
@@ -346,10 +353,11 @@
     for j in range(HS):
         for g in every:
             c = spans[g]
-            force = tq[j, :, c] - cspring[j, :, c] * b[g] - cfric[j, :, c] * a[g]
-            a[g] = a[g] + ratio * product(force, g)
-            force = -cspring[j, :, c] * y[g] - cfric[j, :, c] * u[g]
-            u[g] = u[g] + ratio * product(force, g)
+            known = tq[j, :, c] - cspring[j, :, c] * b[g] - cfric[j, :, c] * a[g]
+            unit = -cspring[j, :, c] * y[g] - cfric[j, :, c] * u[g]
+            gain = ratio * product(jnp.concatenate([unit, known], axis=0), g)
+            u[g] = u[g] + gain[0:DEPTH]
+            a[g] = a[g] + gain[DEPTH:]
         for g in every:
             b[g] = b[g] + ratio * a[g]
             y[g] = y[g] + ratio * u[g]
@@ -365,12 +373,20 @@
         half = 1
         while half < slices:
             for first in range(half, slices, 2 * half):
-                left = spread(ends[first - 1])
+                state = ends[first - 1]
                 for n in range(min(first + half, slices) - 1, first - 1, -1):
-                    ends[n] = ends[n] + apply(left, maps.index[first, n])
+                    right = maps.index[first, n]
+                    target, left = maps.after.get((half, right), (None, None)) if compose else (None, None)
+                    if target is None:
+                        ends[n] = ends[n] + apply(*split(state), right)
+                    else:
+                        both = apply(*split(jnp.concatenate([values[left], state], axis=0)), right)
+                        keep(target, both[0:DEPTH])
+                        ends[n] = ends[n] + both[DEPTH:]
             if compose:
                 for target, left, right in maps.stage[half]:
-                    keep(target, apply(spread(values[left]), right))
+                    if target not in values:
+                        keep(target, apply(*split(values[left]), right))
             half *= 2
         return ends
 
@@ -385,7 +401,7 @@
     unroll = SUB - 1 if len(plan.groups) * SUB <= 256 else 1
     grav = gravity
 
-    def iteration(k, corrections, active, sliced):
+    def iteration(k, active, sliced):
         for n in sliced:
             cut = pl.ds(plan.where[n], DOF)
             ybuf[:, cut] = xs[n, :, 0:DOF]
@@ -433,34 +449,48 @@
             cut = pl.ds(plan.groups[g][0], LANES)
             ybuf[:, cut] = y
             ubuf[:, cut] = u
-        worst = jnp.zeros((epd, 1), F32)
         moved = [packed(ybuf, ubuf, n) - xs[n + 1] if n in sliced else None for n in range(slices)]
         if moved[0] is None:
             moved[0] = jnp.zeros((epd, LANES), F32)
         changes = sweep(moved, None)
         for n in range(slices):
-            real = changes[n] * scale
-            worst = jnp.maximum(worst, jnp.sum(real * real, axis=1, keepdims=True))
+            delta[k, n] = changes[n]
             xs[n + 1] = xs[n + 1] + changes[n]
-        return jnp.where(lane_of == DOF + k, jnp.sqrt(worst), corrections)
 
     groups = range(len(plan.groups))
-    corrections = iteration(0, jnp.zeros((epd, LANES), F32), groups, range(slices))
+    iteration(0, groups, range(slices))
     live = [n for g in plan.later for n in plan.groups[g][1]]
-    corrections = lax.fori_loop(
-        1, ITERS, lambda k, kept: iteration(k, kept, plan.later, live), corrections)
+
+    @pl.loop(1, ITERS)
+    def _(k):
+        iteration(k, plan.later, live)
 
     span = local * epd
     for t in range(tm):
         parts = [xs[t * local + pos + 1] * scale for pos in range(local)]
-        parts[0] = parts[0] + corrections
         turned = jnp.concatenate(parts, axis=0).T
         otx[t, :, 0:span] = turned[0:VOFF]
         otx[t, :, span : 2 * span] = turned[VOFF:DEPTH]
     for c in sends(to_peer(otx), orx.at[me_t], osem, tm, tm_peer):
         c.start()
+    worst = jnp.zeros((high_rows, LANES), F32)
+    for k in range(ITERS):
+        most_moved = jnp.zeros((epd, 1), F32)
+        for n in range(slices):
+            real = delta[k, n] * scale
+            most_moved = jnp.maximum(most_moved, jnp.sum(real * real, axis=1, keepdims=True))
+        corr_t[0:epd, :] = jnp.sqrt(most_moved) + jnp.zeros((epd, LANES), F32)
+        worst = jnp.where(wide_lane == k, corr_t[...], worst)
+    corr_t[...] = worst
+    turned = corr_t[...].T
+    ctx[...] = jnp.zeros(ctx.shape, F32)
+    ctx[:, 0:high_rows] = turned[0:8]
+    for c in sends(lambda k: ctx, crx.at[me_t], csem, tm, tm_peer):
+        c.start()
     orx[me_t] = otx[me_t]
+    crx[me_t] = ctx[...]
     finish(otx.at[most], orx.at[most], osem, tm_peer)
+    finish(crx.at[most], crx.at[most], csem, tm_peer)
 
     across = LANES // epd
     lanes = lax.broadcasted_iota(jnp.int32, (VOFF, LANES), 1)
@@ -476,8 +506,24 @@
                     acc = moved if acc is None else jnp.where(lanes >= q * epd, moved, acc)
                 cut = pl.ds(tile * LANES, LANES)
                 states_out[part * DOF : (part + 1) * DOF, pos, cut] = acc[0:DOF]
-                if part == 0 and pos == 0:
-                    corr_out[:, cut] = acc[DOF : DOF + ITERS]
+    short = lax.broadcasted_iota(jnp.int32, (8, LANES), 1)
+    for tile in range(env_local // LANES):
+        acc = None
+        for q in range(across):
+            moved = moved_to(crx[tile * across + q], q * epd)
+            acc = moved if acc is None else jnp.where(short >= q * epd, moved, acc)
+        corr_out[:, pl.ds(tile * LANES, LANES)] = acc[0:ITERS]
+
+
+def emit(states, corrections, states_out, corr_out, sem):
+    copies = [
+        pltpu.make_async_copy(states, states_out, sem.at[0]),
+        pltpu.make_async_copy(corrections, corr_out, sem.at[1]),
+    ]
+    for c in copies:
+        c.start()
+    for c in copies:
+        c.wait()
 
 
 def body(tm, env, init_state, torque, contact, mass_inverse, stiffness, damping, gravity,
@@ -527,12 +573,27 @@
             pltpu.VMEM((DEPTH, lanes), F32), pltpu.VMEM((DEPTH, lanes), F32),
             pltpu.VMEM((maps, WIDE, LANES), BF16),
             pltpu.VMEM((slices + 1, epd, LANES), F32),
-            dma((2,)), dma((2,)), dma((2,)), dma((2,)), dma((9,)),
+            dma((2,)), dma((2,)), dma((2,)), dma((2,)), dma((2,)), dma((9,)),
+            pltpu.VMEM((ITERS, slices, epd, LANES), F32),
+            pltpu.VMEM((up8(epd), LANES), F32),
+            pltpu.VMEM((8, LANES), F32), pltpu.VMEM((tm, 8, LANES), F32),
         ],
         compiler_params=pltpu.CompilerParams(collective_id=0, has_side_effects=True),
         name="parareal",
     )(contact, jnp.transpose(torque, (1, 0, 2)),
       jnp.transpose(mass_inverse, (1, 0, 2)), init_state, *prm)
+    states, corrections = pl.pallas_call(
+        emit,
+        out_shape=(
+            jax.ShapeDtypeStruct(states.shape, F32),
+            jax.ShapeDtypeStruct(corrections.shape, F32),
+        ),
+        in_specs=[vmem] * 2,
+        out_specs=[pl.BlockSpec(memory_space=pl.ANY)] * 2,
+        scratch_shapes=[dma((2,))],
+        name="emit",
+    )(pltpu.with_memory_space_constraint(states, pltpu.VMEM),
+      pltpu.with_memory_space_constraint(corrections, pltpu.VMEM))
     return jnp.transpose(states, (1, 0, 2)), corrections
 
 

time: 52.7 us -> 52 us (0.987)
  local copies, waits for them, and re-layouts: 1.25 us -> 0 us
    unnamed x2 -> x0, local copies, waits for them, and re-layouts: 1.25 us -> none
    pallas_call x0 -> x1, Pallas kernels: none -> 0.68 us  [body(): pl.pallas_call(emit, out_shape=(jax.ShapeDtypeStruct(states.shape, F32),...]
where the time goes in v4:
time: 52 us; the launch traced here: 51.8 us
  Pallas kernels  51 us (98%)
  between operations  0.8 us (2%)
    pallas_call x1, Pallas kernels, body(): pl.pallas_call(functools.partial(kernel, tm, env, local, env_local * env)...  50.3 us

profile of v4, /device:TPU:0, one launch (start us, length us, event | category | flops | bytes accessed | tf_op | source)
XLA Modules:
  0.0 51.8 jit_solution(12929162936755157316)
XLA Ops:
  0.6 50.3 %parareal.1 = (f32[70,2,256]{2,1,0:T(2,128)S(1)}, f32[3,256]{1,0:T(4,128)S(1)}) custom-call(s32[4,256]{1,0:T(4,128)} %contact_h.1, f32[35,4,256]{2,1,0:T(4,128)} %bitcast.8, f32[35,2,35]{2,1,0:T(2,128)} %bitcast.9, f32[70,256]{1,0:T(8,128)} %init_h.1, f32[1,35]{1,0:T(1,128)} %bitcast.10, f32[1,35]{1,0:T(1,128)} %bitcast.11, f32[1,35]{1,0:T(1,128)} %bitcast.12, ...), custom_call_target="tpu_custom_call" | custom-call | tf_op jit(solution)/shard_map/parareal/pallas_call | solution.py:548
  50.9 0.7 %emit.1 = (f32[70,2,256]{2,1,0:T(2,128)}, f32[3,256]{1,0:T(4,128)}) custom-call(f32[70,2,256]{2,1,0:T(2,128)S(1)} %get-tuple-element.6.states, f32[3,256]{1,0:T(4,128)S(1)} %get-tuple-element.7.corrections), custom_call_target="tpu_custom_call" | custom-call | tf_op jit(solution)/shard_map/emit/pallas_call | solution.py:585

commit v5 on v4

--- a/solution.py
+++ b/solution.py
@@ -374,6 +374,8 @@
         while half < slices:
             for first in range(half, slices, 2 * half):
                 state = ends[first - 1]
+                if state is None:
+                    continue
                 for n in range(min(first + half, slices) - 1, first - 1, -1):
                     right = maps.index[first, n]
                     target, left = maps.after.get((half, right), (None, None)) if compose else (None, None)
@@ -399,7 +401,7 @@
         xs[n + 1] = ends[n]
 
     unroll = SUB - 1 if len(plan.groups) * SUB <= 256 else 1
-    grav = gravity
+    load = [c * gravity for c in SIN]
 
     def iteration(k, active, sliced):
         for n in sliced:
@@ -422,12 +424,11 @@
                     base = ahead - jnp.round(ahead)
                     s = t * t
                     s2 = s * s
-                    weight = grav * t
-                    weight2 = weight * s2
+                    weight2 = t * s2
                     linear = ((tq[j, :, cut] + rest) - spring[j, :, cut] * y) - fric[j, :, cut] * u
-                    force = linear - weight * (SIN[1] * s + SIN[0])
-                    force = force - weight2 * (SIN[3] * s + SIN[2])
-                    force = force - (weight2 * s2) * (SIN[5] * s + SIN[4])
+                    force = linear - t * (load[1] * s + load[0])
+                    force = force - weight2 * (load[3] * s + load[2])
+                    force = force - (weight2 * s2) * (load[5] * s + load[4])
                     sent = force.astype(BF16)
                     rest = force - sent.astype(F32)
                     push = once(sent, g)
@@ -438,7 +439,7 @@
                 return tuple(result)
 
             carry = lax.fori_loop(0, SUB - 1, functools.partial(substep, False), carry, unroll=unroll)
-            return substep(True, SUB - 1, carry)
+            return substep(not isinstance(j, int) or j == HS - 1, SUB - 1, carry)
 
         if unroll > 1:
             for j in range(HS):
@@ -450,10 +451,11 @@
             ybuf[:, cut] = y
             ubuf[:, cut] = u
         moved = [packed(ybuf, ubuf, n) - xs[n + 1] if n in sliced else None for n in range(slices)]
-        if moved[0] is None:
-            moved[0] = jnp.zeros((epd, LANES), F32)
-        changes = sweep(moved, None)
+        changes = sweep(moved)
         for n in range(slices):
+            if changes[n] is None:
+                delta[k, n] = jnp.zeros((epd, LANES), F32)
+                continue
             delta[k, n] = changes[n]
             xs[n + 1] = xs[n + 1] + changes[n]
 

time: 52 us -> 51.6 us (level)
  no operation moved by 1% of the time
where the time goes in v5:
time: 51.6 us; the launch traced here: 51.4 us
  Pallas kernels  50.6 us (98%)
  between operations  0.8 us (2%)
    pallas_call x1, Pallas kernels, body(): pl.pallas_call(functools.partial(kernel, tm, env, local, env_local * env)...  50 us

profile of v5, /device:TPU:0, one launch (start us, length us, event | category | flops | bytes accessed | tf_op | source)
XLA Modules:
  0.0 51.4 jit_solution(3591530725105729688)
XLA Ops:
  0.6 50.0 %parareal.1 = (f32[70,2,256]{2,1,0:T(2,128)S(1)}, f32[3,256]{1,0:T(4,128)S(1)}) custom-call(s32[4,256]{1,0:T(4,128)} %contact_h.1, f32[35,4,256]{2,1,0:T(4,128)} %bitcast.8, f32[35,2,35]{2,1,0:T(2,128)} %bitcast.9, f32[70,256]{1,0:T(8,128)} %init_h.1, f32[1,35]{1,0:T(1,128)} %bitcast.10, f32[1,35]{1,0:T(1,128)} %bitcast.11, f32[1,35]{1,0:T(1,128)} %bitcast.12, ...), custom_call_target="tpu_custom_call" | custom-call | tf_op jit(solution)/shard_map/parareal/pallas_call | solution.py:550
  50.6 0.7 %emit.1 = (f32[70,2,256]{2,1,0:T(2,128)}, f32[3,256]{1,0:T(4,128)}) custom-call(f32[70,2,256]{2,1,0:T(2,128)S(1)} %get-tuple-element.6.states, f32[3,256]{1,0:T(4,128)S(1)} %get-tuple-element.7.corrections), custom_call_target="tpu_custom_call" | custom-call | tf_op jit(solution)/shard_map/emit/pallas_call | solution.py:587
